TPU v7x, 128 devices: a whole 4x4x4 slice. The times are simulated.
128 devices in a mesh: dp: 16 (over z, y), expert: 8 (over x, core).
Axes of the slice: x: 4, y: 4, z: 4, core: 2. Of those that a mesh axis runs over, the one named last changes fastest.
Arguments:
- tokens: bfloat16 [2048, 4096], P('dp'), may hold values from -6 to 6
- expert_ids: int32 [2048, 2], P('dp'), may hold values from 0 to 7, all different within a row; in each aligned block of 128 rows (0 to 127, 128 to 255, ...) at most 96 rows name the same one
- gate_weights: float32 [2048, 2], P('dp'), may hold values from 0.2 to 1
- live_counts: int32 [16], P('dp'), may hold values from 64 to 128, as said below
- w_gate: bfloat16 [8, 4096, 8192], P('expert', None, 'dp'), may hold values from -0.09375 to 0.09375
- w_up: bfloat16 [8, 4096, 8192], P('expert', None, 'dp'), may hold values from -0.09375 to 0.09375
- w_down: bfloat16 [8, 8192, 4096], P('expert', 'dp'), may hold values from -0.0625 to 0.0625
Outputs:
- mixed: bfloat16 [2048, 4096], P('dp')
- total_loads: int32 [8], replicated
Inputs may be any that keep to these rules, and one draw needn't show every extreme that they name: `expert_ids`: each token names two different experts. Among the tokens of one rank no expert is named more than 96 times, a bound that some block reaches in some ranks. Rank r's first live_counts[r] tokens are live, the rest are padding. Some rank has all 128 tokens live.
All inputs are finite; a program needn't handle non-finite values.
Results may differ from a plain program's by a relative error of at most 0.017.
Values may be sent and summed in bfloat16 or wider, within the bound.
A program may use at most 128 MiB of HBM per device.

v0:
```python
import jax
import jax.numpy as jnp
from jax import lax
from jax.sharding import Mesh
from jax.sharding import PartitionSpec as P

DP = ("dp_0", "dp_1")


def split_up(shard, dim, size):
    before, after = (shard.shape[:dim], shard.shape[dim + 1 :])
    return jnp.moveaxis(shard.reshape(*before, size, -1, *after), dim, 0)


def sum_at_owner(shard, axis, dim):
    size = lax.axis_size(axis)
    tiles = lax.all_to_all(split_up(shard, dim, size), axis, 0, 0, tiled=True)
    return jnp.sum(tiles.astype(jnp.float32), axis=0)


def from_everyone(shard, axis):
    copies = jnp.broadcast_to(shard, (lax.axis_size(axis), *shard.shape))
    return lax.all_to_all(copies, axis, split_axis=0, concat_axis=0, tiled=True)


def laid_out(tiles, dim):
    dims = list(tiles.shape[1:])
    dims[dim] *= tiles.shape[0]
    return jnp.moveaxis(tiles, 0, dim).reshape(dims)


def gather_directly(shard, axis, dim):
    tiles = from_everyone(shard, axis)
    return laid_out(tiles, dim)


def over_axes(shard, axes):
    for axis in axes:
        shard = lax.psum(shard, axis)
    return shard


def plan_routes(expert_ids, live_total, n_experts, capacity):
    row_count = expert_ids.shape[0]
    is_live = jnp.arange(row_count, dtype=jnp.int32) < live_total
    flat_ids = expert_ids.reshape(-1)
    live_pairs = jnp.repeat(is_live, 2)
    one_hot = (
        (flat_ids[:, None] == jnp.arange(n_experts, dtype=jnp.int32)[None, :]) & live_pairs[:, None]
    ).astype(jnp.int32)
    earlier = jnp.cumsum(one_hot, axis=0) - one_hot
    slot_index = jnp.sum(earlier * one_hot, axis=1)
    targets = jnp.where(live_pairs, flat_ids * capacity + slot_index, -1)
    return (targets.reshape(row_count, 2), jnp.sum(one_hot, axis=0))


def dispatch_rows(tokens, targets, slots_all):
    wanted = targets.reshape(-1)[None, :] == jnp.arange(slots_all, dtype=jnp.int32)[:, None]
    wanted = jnp.any(wanted.reshape(slots_all, -1, 2), axis=2).astype(jnp.bfloat16)
    return jnp.dot(wanted, tokens, preferred_element_type=jnp.float32).astype(jnp.bfloat16)


def per_device(tokens, expert_ids, gate_weights, live_counts, w_gate, w_up, w_down):
    n_experts = lax.axis_size("expert")
    my_expert = lax.axis_index("expert")
    capacity = 3 * tokens.shape[0] // 4
    targets, expert_loads = plan_routes(expert_ids, live_counts[0], n_experts, capacity)
    local_slots = targets - my_expert * capacity
    outbound = dispatch_rows(tokens, local_slots, capacity)
    gathered = lax.all_gather(outbound, DP, axis=0, tiled=True)
    gate_matrix = w_gate[0]
    up_matrix = w_up[0]
    down_matrix = w_down[0]
    gate_act = jnp.dot(gathered, gate_matrix, preferred_element_type=jnp.float32)
    up_act = jnp.dot(gathered, up_matrix, preferred_element_type=jnp.float32)
    hidden = (jax.nn.silu(gate_act) * up_act).astype(jnp.bfloat16)
    summed = lax.psum_scatter(
        jnp.dot(hidden, down_matrix, preferred_element_type=jnp.float32).astype(jnp.bfloat16),
        DP,
        scatter_dimension=0,
        tiled=True,
    )
    is_mine = (local_slots >= 0) & (local_slots < capacity)
    pick_index = jnp.where(is_mine, local_slots, 0)
    selected = summed[pick_index].astype(jnp.float32)
    weights = jnp.where(is_mine, gate_weights, jnp.zeros_like(gate_weights))
    weighted = jnp.sum(weights[:, :, None] * selected, axis=1)
    share = sum_at_owner(weighted.astype(jnp.bfloat16), "expert", 0).astype(jnp.bfloat16)
    mixed = gather_directly(share, "expert", 0)
    total_loads = over_axes(expert_loads, DP)
    return (mixed, total_loads)


def solution(mesh):
    torus = Mesh(mesh.devices.reshape(4, 4, mesh.shape["expert"]), ("dp_0", "dp_1", "expert"))
    in_specs = (
        P(DP, None),
        P(DP, None),
        P(DP, None),
        P(DP),
        P("expert", None, DP),
        P("expert", None, DP),
        P("expert", DP, None),
    )
    out_specs = (P(DP, None), P())
    return jax.shard_map(
        per_device, mesh=torus, in_specs=in_specs, out_specs=out_specs, check_vma=False
    )
```

profile of v0, /device:TPU:1, one launch (start us, length us, event | category | flops | bytes accessed | tf_op | source)
XLA Modules:
  0.0 302.1 jit_solution(7526284278638504880)
XLA Ops:
  7.2 0.8 broadcast_multiply_fusion
  8.0 0.8 copy.17
  9.8 0.1 broadcast_in_dim.27
  10.1 0.1 and.20
  10.3 0.6 reduce-window.6
  10.9 0.2 slice_reduce_fusion
  11.2 0.1 convert_reduce_fusion
  11.5 0.8 copy.20
  12.5 1.2 convolution_convert_fusion.1
  13.8 93.1 %all-gather.2.cloned.1.call-done = bf16[1536,4096]{1,0:T(8,128)(2,1)} async-done(((bf16[96,4096]{1,0:T(8,128)(2,1)}), bf16[1536,4096]{1,0:T(8,128)(2,1)}) %all-gather.2.cloned.1.call-update) | async-done | bytes 12582928 | tf_op jit(solution)/shard_map/all_gather | solution.py:70
  106.9 12.0 %fusion.3 = f32[1536,512]{1,0:T(8,128)} fusion(bf16[1536,4096]{1,0:T(8,128)(2,1)} %all-gather.2.cloned.1.call-done, bf16[1,4096,512]{2,1,0:T(8,128)(2,1)} %param.11), kind=kOutput, calls=%fused_computation.6 | convolution fusion | flops 6442450944 | bytes 19922944 | tf_op jit(solution)/shard_map/dot_general | solution.py:74
  118.8 21.9 %convolution_convert_fusion = bf16[1536,4096]{1,0:T(8,128)(2,1)} fusion(bf16[1,512,4096]{2,1,0:T(8,128)(2,1)} %param.13, bf16[1536,4096]{1,0:T(8,128)(2,1)} %all-gather.2.cloned.1.call-done, bf16[1,4096,512]{2,1,0:T(8,128)(2,1)} %param.12, f32[1536,512]{1,0:T(8,128)} %fusion.3), kind=kOutput, calls=%fused_computation.1 | convolution fusion | flops 12895911936 | bytes 36700160 | tf_op jit(solution)/shard_map/dot_general | solution.py:78
  140.9 94.7 %reduce-scatter.2.cloned.1.call-done = bf16[96,4096]{1,0:T(8,128)(2,1)} async-done(((bf16[1536,4096]{1,0:T(8,128)(2,1)}), bf16[96,4096]{1,0:T(8,128)(2,1)}) %reduce-scatter.2.cloned.1.call-update) | async-done | bytes 786448 | tf_op jit(solution)/shard_map/reduce_scatter | solution.py:77
  235.6 5.1 %gather_fusion = bf16[256,4096]{1,0:T(8,128)(2,1)S(1)} fusion(bf16[96,4096]{1,0:T(8,128)(2,1)} %reduce-scatter.2.cloned.1.call-done, s32[1024]{0:T(1024)S(1)} %pad_clamp_fusion), kind=kCustom, calls=%fused_computation | custom fusion | bytes 4195328 | tf_op jit(solution)/shard_map/gather | solution.py:85
  240.8 4.0 %reshape.63 = f32[128,2,4096]{2,1,0:T(2,128)} reshape(bf16[256,4096]{1,0:T(8,128)(2,1)S(1)} %gather_fusion) | data formatting | bytes 6291456 | tf_op jit(solution)/shard_map/convert_element_type | solution.py:85
  244.8 8.7 %multiply_reduce_fusion = bf16[128,4096]{1,0:T(8,128)(2,1)S(1)} fusion(f32[128,2,4096]{2,1,0:T(2,128)} %reshape.63, f32[128,2]{1,0:T(8,128)S(1)} %get-tuple-element.4), kind=kLoop, calls=%fused_computation.8 | loop fusion | flops 1572864 | bytes 5243904 | tf_op jit(solution)/shard_map/reduce_sum | solution.py:87
  253.4 20.2 %all_to_all.10 = bf16[8,16,4096]{2,1,0:T(8,128)(2,1)S(1)} all-to-all(bf16[8,16,4096]{2,1,0:T(8,128)(2,1)S(1)} %bitcast.29), channel_id=1, replica_groups=mesh['dp_0'=4,'dp_1'=4,'expert'=8] {'expert'}, dimensions={0} | all-to-all | bytes 2097152 | tf_op jit(solution)/shard_map/all_to_all | solution.py:17
  273.6 0.1 reduce_sum.44
  273.7 1.1 broadcast_in_dim.31
  274.8 4.5 %all-to-all-start.1 = ((bf16[8,16,4096]{2,1,0:T(8,128)(2,1)}), bf16[8,16,4096]{2,1,0:T(8,128)(2,1)S(1)}, u32[]{:S(2)}, u32[]{:S(2)}) async-start(bf16[8,16,4096]{2,1,0:T(8,128)(2,1)} %broadcast_in_dim.31), calls=%async_computation.2 | async-start | bytes 2097152 | tf_op jit(solution)/shard_map/all_to_all | solution.py:23
  279.3 6.5 %psum.14 = s32[8]{0:T(128)S(1)} all-reduce(s32[8]{0:T(128)S(1)} %get-tuple-element.2), channel_id=1, replica_groups=mesh['dp_0'=4,'dp_1'=4,'expert'=8] {'dp_0'}, use_global_device_ids=true, to_apply=%region_8.9 | all-reduce | flops 8 | bytes 64 | tf_op jit(solution)/shard_map/psum | solution.py:39
  285.8 6.1 %psum.15 = s32[8]{0:T(128)} all-reduce(s32[8]{0:T(128)S(1)} %psum.14), channel_id=1, replica_groups=mesh['dp_0'=4,'dp_1'=4,'expert'=8] {'dp_1'}, use_global_device_ids=true, to_apply=%region_9.10 | all-reduce | flops 8 | bytes 64 | tf_op jit(solution)/shard_map/psum | solution.py:39
  291.9 2.4 all-to-all-done.1
  294.3 1.0 copy.25
  (23 shorter events, 1.2 us)
Async XLA Ops:
  7.2 5.3 %copy-start = (bf16[128,4096]{1,0:T(8,128)(2,1)S(1)}, bf16[128,4096]{1,0:T(8,128)(2,1)}, u32[]{:S(2)}) copy-start(bf16[128,4096]{1,0:T(8,128)(2,1)} %param.7) | copy-start | bytes 3145732
  7.2 99.7 %all-gather.2.cloned.1.call-start = ((), (), s32[]{:S(2)}) async-start(), calls=%async_computation.3 | async-start | bytes 13369344 | tf_op jit(solution)/shard_map/all_gather | solution.py:70
  13.8 221.9 %reduce-scatter.2.cloned.1.call-start = ((), (), s32[]{:S(2)}) async-start(), calls=%async_computation.4 | async-start | bytes 13369344 | tf_op jit(solution)/shard_map/reduce_scatter | solution.py:77
  274.8 19.5 %all-to-all-start.1 = ((bf16[8,16,4096]{2,1,0:T(8,128)(2,1)}), bf16[8,16,4096]{2,1,0:T(8,128)(2,1)S(1)}, u32[]{:S(2)}, u32[]{:S(2)}) async-start(bf16[8,16,4096]{2,1,0:T(8,128)(2,1)} %broadcast_in_dim.31), calls=%async_computation.2 | async-start | bytes 2097152 | tf_op jit(solution)/shard_map/all_to_all | solution.py:23
Sparse Core Ops, SparseCore 0:
  13.9 92.9 all-gather.1
  140.8 94.7 reduce-scatter.1
where the time goes:
time: 303 us; the launch traced here: 302 us
  waiting for transfers between devices  190 us (63%)
  matrix products  35.1 us (12%)
  blocking collectives  32.7 us (11%)
  between operations  14.8 us (5%)
  local copies, waits for them, and re-layouts  14.1 us (5%)
  other arithmetic  10.5 us (3%)
  starting transfers between devices  4.58 us (2%)
    reduce_scatter x1, waiting for transfers between devices, per_device(): lax.psum_scatter(jnp.dot(hidden, down_matrix, preferred_element_type=jnp....  94.7 us
    all_gather x1, waiting for transfers between devices, per_device(): gathered = lax.all_gather(outbound, DP, axis=0, tiled=True)  93.1 us
    dot_general x1, matrix products, per_device(): jnp.dot(hidden, down_matrix, preferred_element_type=jnp.float32)  21.9 us
    all_to_all x1, blocking collectives, sum_at_owner(): tiles = lax.all_to_all(split_up(shard, dim, size), axis, 0, 0, tiled=True)  20.2 us
    psum x2, blocking collectives, over_axes(): shard = lax.psum(shard, axis)  12.6 us
    dot_general x1, matrix products, per_device(): jnp.dot(gathered, gate_matrix, preferred_element_type=jnp.float32)  12 us
    reduce_sum x1, other arithmetic, per_device(): weighted = jnp.sum(weights[:, :, None] * selected, axis=1)  8.66 us
  transfers between devices with their start and end apart: 3, of which 3 were waited for; matrix products, arithmetic and copies ran while one was open for 0% of the time, Pallas kernels for 0%

commit v1 on v0

v1 whole, which is shorter than its diff:
```python
import functools
import jax
import jax.numpy as jnp
from jax import lax
from jax.experimental import pallas as pl
from jax.experimental.pallas import tpu as pltpu
from jax.sharding import Mesh
from jax.sharding import PartitionSpec as P

MESH = pl.DeviceIdType.MESH
DP = ("z", "y")
EXPERT = ("x", "c")
RINGS = (("y", "z"), ("z", "y"))
VMEM_LIMIT = 67043328


def shifted(axis, by):
    return lax.rem(lax.axis_index(axis) + by % 4, 4)


def other_core():
    return {"c": 1 - lax.axis_index("c")}


class Sender:
    def __init__(self, sems):
        self.sems, self.copies = sems, []

    def __call__(self, src, dst, recv_sem, where):
        copy = pltpu.make_async_remote_copy(
            src_ref=src,
            dst_ref=dst,
            send_sem=self.sems.at[len(self.copies)],
            recv_sem=recv_sem,
            device_id=where,
            device_id_type=MESH,
        )
        copy.start()
        self.copies.append(copy)

    def drain(self):
        for copy in self.copies:
            copy.wait_send()


def landed(ref, sem):
    pltpu.make_async_copy(ref, ref, sem).wait()


def enter(peers):
    barrier = pltpu.get_barrier_semaphore()
    for peer in peers:
        pl.semaphore_signal(barrier, inc=1, device_id=peer, device_id_type=MESH)
    pl.semaphore_wait(barrier, len(peers))


def gather_kernel(
    tok, meta, wg_hbm, wu_hbm, hid, loads, x, wg, wu, m, wcol, wsem, send_sem, blk_sem, half_sem, swap_sem, meta_sem
):
    c = lax.axis_index("c")
    expert = lax.axis_index("x") * 2 + c
    loads_in = [pltpu.make_async_copy(wg_hbm, wg, wsem.at[0]), pltpu.make_async_copy(wu_hbm, wu, wsem.at[1])]
    for copy in loads_in:
        copy.start()
    rows = x.shape[4]
    half = rows // 2
    peers = [(i, j) for i in range(4) for j in range(4) if (i, j) != (0, 0)]
    enter([other_core()] + [{"z": shifted("z", i), "y": shifted("y", j)} for i, j in peers])
    send = Sender(send_sem)

    def own_rows(h, o):
        owner = c if o == 0 else 1 - c
        return pl.ds(pl.multiple_of(owner * (2 * rows) + h * rows, rows), rows)

    for h in range(2):
        mine = tok.at[own_rows(h, 0)]
        a1, a2 = RINGS[h]
        send(mine, x.at[h, 0, 0, 3], blk_sem.at[h, 0, 3], {a1: shifted(a1, 1)})
        send(mine, x.at[h, 0, 0, 1], blk_sem.at[h, 0, 1], {a1: shifted(a1, -1)})
    for h in range(2):
        mine = tok.at[own_rows(h, 0)]
        a1, a2 = RINGS[h]
        send(mine, x.at[h, 3, 0, 0], blk_sem.at[h, 3, 0], {a2: shifted(a2, 1)})
        send(mine, x.at[h, 1, 0, 0], blk_sem.at[h, 1, 0], {a2: shifted(a2, -1)})
    for i, j in peers:
        at = (-i % 4, -j % 4)
        send(meta, m.at[at], meta_sem.at[at], {"z": shifted("z", i), "y": shifted("y", j)})
    m[0, 0] = meta[...]
    for h in range(2):
        for o in range(2):
            x[h, 0, o, 0] = tok[own_rows(h, o), :]

    def swap(h, g, b):
        send(x.at[h, g, 0, b], x.at[h, g, 1, b], swap_sem.at[h, g, b], other_core())

    def spread(h, b):
        a2 = RINGS[h][1]
        send(x.at[h, 0, 0, b], x.at[h, 3, 0, b], blk_sem.at[h, 3, b], {a2: shifted(a2, 1)})
        send(x.at[h, 0, 0, b], x.at[h, 1, 0, b], blk_sem.at[h, 1, b], {a2: shifted(a2, -1)})
        swap(h, 0, b)

    def near(h):
        a1 = RINGS[h][0]
        for b, step, part in ((3, 1, 0), (1, -1, 1)):
            landed(x.at[h, 0, 0, b], blk_sem.at[h, 0, b])
            piece = pl.ds(part * half, half)
            send(
                x.at[h, 0, 0, b, piece], x.at[h, 0, 0, 2, piece], half_sem.at[h, part], {a1: shifted(a1, step)}
            )
            spread(h, b)

    def far(h):
        for part in range(2):
            landed(x.at[h, 0, 0, 2, pl.ds(part * half, half)], half_sem.at[h, part])
        spread(h, 2)

    def onward(h, b):
        a2 = RINGS[h][1]
        for g, step, passes in ((3, 1, (0, 2)), (1, -1, (3, 1))):
            landed(x.at[h, g, 0, b], blk_sem.at[h, g, b])
            if b in passes:
                send(x.at[h, g, 0, b], x.at[h, 2, 0, b], blk_sem.at[h, 2, b], {a2: shifted(a2, step)})
            swap(h, g, b)

    def last(h, b):
        landed(x.at[h, 2, 0, b], blk_sem.at[h, 2, b])
        swap(h, 2, b)

    def weigh():
        for i, j in peers:
            landed(m.at[i, j], meta_sem.at[i, j])
        total = jnp.zeros(m.shape[2:], jnp.float32)
        for i in range(4):
            for j in range(4):
                total = total + jnp.where(m[i, j] > 0.0, 1.0, 0.0)
                row = m[i, j, pl.ds(expert, 1), :]
                wcol[i, j] = jnp.transpose(jnp.broadcast_to(row, (row.shape[1], row.shape[1])))
        loads[...] = jnp.broadcast_to(jnp.sum(total, axis=1, keepdims=True), loads.shape).astype(jnp.int32)

    def compute(h, g):
        for b in range(4):
            if (g, b) != (0, 0):
                landed(x.at[h, g, 1, b], swap_sem.at[h, g, b])
        parts = []
        for o in range(2):
            for b in range(4):
                at = (g, b) if h == 0 else (b, g)
                parts.append(wcol[at[0], at[1], own_rows(h, o), :])
        weight = jnp.concatenate(parts, axis=0)
        weight = jnp.concatenate([weight, weight], axis=1)

        @pl.loop(0, 2)
        def _(n):
            cols = pl.ds(pl.multiple_of(n * 256, 256), 256)
            lhs = x[h, g].reshape(8 * rows, x.shape[5])
            gate = jnp.dot(lhs, wg[:, cols], preferred_element_type=jnp.float32)
            up = jnp.dot(lhs, wu[:, cols], preferred_element_type=jnp.float32)
            act = gate / (1.0 + jnp.exp(-gate)) * up * weight
            hid[h, g, :, cols] = act.astype(jnp.bfloat16)

    near(0), near(1)
    onward(0, 0), onward(1, 0)
    far(0), far(1)
    weigh()
    for copy in loads_in:
        copy.wait()
    compute(0, 0)
    onward(0, 3), onward(1, 3)
    compute(1, 0)
    onward(0, 1), onward(1, 1)
    last(0, 0), last(1, 0)
    onward(0, 2), onward(1, 2)
    compute(0, 3)
    last(0, 3), last(1, 3)
    compute(0, 1)
    last(0, 1), last(1, 1)
    compute(1, 3)
    compute(1, 1)
    last(0, 2), last(1, 2)
    compute(0, 2)
    compute(1, 2)
    send.drain()


def scatter_kernel(
    hid, wd_hbm, out, wd, s, p, l, f, n1, t, f2, n2, r, xr, ob, wsem, send_sem, l_sem, f_sem, n_sem, f2_sem, n2_sem,
    x_sem, ox_sem, od_sem, out_sem,
):
    c, xi = lax.axis_index("c"), lax.axis_index("x")
    load = pltpu.make_async_copy(wd_hbm, wd, wsem)
    load.start()
    rows, width = s.shape[3], s.shape[4]
    half = rows // 2
    enter(
        [other_core()]
        + [{a: shifted(a, by)} for a in ("y", "z") for by in (1, -1)]
        + [{"x": shifted("x", by)} for by in (1, 2, 3)]
    )
    send = Sender(send_sem)
    load.wait()
    f32 = lambda v: v.astype(jnp.float32)
    bf16 = lambda v: v.astype(jnp.bfloat16)

    def compute(h, g):
        @pl.loop(0, width // 512)
        def _(n):
            cols = pl.ds(pl.multiple_of(n * 512, 512), 512)
            y = bf16(jnp.dot(hid[h, g], wd[:, cols], preferred_element_type=jnp.float32))
            s[h, g, :, :, cols] = y[: 4 * rows].reshape(4, rows, 512)
            p[h, g, :, :, cols] = y[4 * rows :].reshape(4, rows, 512)

        send(p.at[h, g], l.at[h, g], l_sem.at[h, g], other_core())

    def chip_sum(h, g):
        landed(l.at[h, g], l_sem.at[h, g])

        @pl.loop(0, 4)
        def _(b):
            s[h, g, b] = bf16(f32(s[h, g, b]) + f32(l[h, g, b]))

    ways = ((1, 0, (2, 0)), (-1, 1, (1, 3)))

    def send_far(h):
        a2 = RINGS[h][1]
        for k in range(2):
            for step, way, blocks in ways:
                b = blocks[k]
                send(s.at[h, 2, b], f.at[h, way, k], f_sem.at[h, way, k], {a2: shifted(a2, step)})

    def send_near(h, way):
        a2 = RINGS[h][1]
        step, _, blocks = ways[way]
        g = 1 if way == 0 else 3
        for b in (2, 1, 3, 0):
            if b not in blocks:
                send(s.at[h, g, b], n1.at[h, way, b], n_sem.at[h, way, b], {a2: shifted(a2, step)})

    def pass_on(h, k):
        a2 = RINGS[h][1]
        for step, way, blocks in ways:
            b = blocks[k]
            g = 1 if way == 0 else 3
            landed(f.at[h, way, k], f_sem.at[h, way, k])
            s[h, g, b] = bf16(f32(s[h, g, b]) + f32(f[h, way, k]))
            send(s.at[h, g, b], n1.at[h, way, b], n_sem.at[h, way, b], {a2: shifted(a2, step)})

    def collect(h, b):
        for way in range(2):
            landed(n1.at[h, way, b], n_sem.at[h, way, b])
        t[h, b] = bf16(f32(s[h, 0, b]) + f32(n1[h, 0, b]) + f32(n1[h, 1, b]))

    def send_far2(h):
        a1 = RINGS[h][0]
        for step, way in ((1, 0), (-1, 1)):
            send(t.at[h, 2, pl.ds(way * half, half)], f2.at[h, way], f2_sem.at[h, way], {a1: shifted(a1, step)})

    def pass_on2(h):
        a1 = RINGS[h][0]
        for step, way in ((1, 0), (-1, 1)):
            b = 1 if way == 0 else 3
            piece = pl.ds(way * half, half)
            landed(f2.at[h, way], f2_sem.at[h, way])
            t[h, b, piece] = bf16(f32(t[h, b, piece]) + f32(f2[h, way]))
            send(t.at[h, b], n2.at[h, way], n2_sem.at[h, way], {a1: shifted(a1, step)})

    def finish_plane(h):
        for way in range(2):
            landed(n2.at[h, way], n2_sem.at[h, way])
        for part in range(2):
            piece = pl.ds(part * half, half)
            r[2 * h + part] = bf16(f32(t[h, 0, piece]) + f32(n2[h, 0, piece]) + f32(n2[h, 1, piece]))

    compute(0, 2)
    compute(1, 2)
    chip_sum(0, 2)
    send_far(0)
    compute(0, 1)
    chip_sum(1, 2)
    send_far(1)
    compute(0, 3)
    chip_sum(0, 1)
    send_near(0, 0)
    compute(1, 1)
    chip_sum(0, 3)
    send_near(0, 1)
    compute(1, 3)
    chip_sum(1, 1)
    send_near(1, 0)
    pass_on(0, 0)
    compute(0, 0)
    chip_sum(1, 3)
    send_near(1, 1)
    pass_on(1, 0)
    compute(1, 0)
    chip_sum(0, 0)
    chip_sum(1, 0)
    pass_on(0, 1), pass_on(1, 1)
    for b in (2, 1, 3, 0):
        for h in range(2):
            collect(h, b)
            if b == 2:
                send_far2(h)
    pass_on2(0), pass_on2(1)
    finish_plane(0), finish_plane(1)

    for by in (1, 2, 3):
        send(r.at[lax.rem(xi + by, 4)], xr.at[by - 1], x_sem.at[by - 1], {"x": shifted("x", by)})
    total = f32(r[xi])
    for by in (1, 2, 3):
        landed(xr.at[by - 1], x_sem.at[by - 1])
        total = total + f32(xr[by - 1])
    ob[c, xi] = bf16(total)
    for by in (1, 2, 3):
        send(ob.at[c, xi], ob.at[c, xi], ox_sem.at[by - 1], {"x": shifted("x", by)})
    send(ob.at[c, xi], ob.at[c, xi], od_sem.at[0], other_core())
    for by in (1, 2, 3):
        source = lax.rem(xi + 4 - by, 4)
        landed(ob.at[c, source], ox_sem.at[by - 1])
        send(ob.at[c, source], ob.at[c, source], od_sem.at[by], other_core())
    for by in range(4):
        landed(ob.at[1 - c, lax.rem(xi + 4 - by, 4)], od_sem.at[by])
    store = pltpu.make_async_copy(ob, out, out_sem)
    store.start()
    store.wait()
    send.drain()


def per_device(tokens, expert_ids, gate_weights, live_counts, w_gate, w_up, w_down):
    count, width = tokens.shape
    depth = w_gate.shape[2]
    rows = count // 4
    dma = pltpu.SemaphoreType.DMA
    bf16, f32 = jnp.bfloat16, jnp.float32
    is_live = jnp.arange(count, dtype=jnp.int32)[None, :] < live_counts[0]
    ids, gates = expert_ids.T, gate_weights.T
    named = (ids[:, None, :] == jnp.arange(8, dtype=jnp.int32)[None, :, None]) & is_live[None]
    meta = jnp.sum(jnp.where(named, gates[:, None, :], 0.0), axis=0)

    vmem = pl.BlockSpec(memory_space=pltpu.VMEM)
    hbm = pl.BlockSpec(memory_space=pl.ANY)
    hidden, loads = pl.pallas_call(
        gather_kernel,
        out_shape=(jax.ShapeDtypeStruct((2, 4, 8 * rows, depth), bf16), jax.ShapeDtypeStruct((8, 128), jnp.int32)),
        in_specs=[vmem, vmem, hbm, hbm],
        out_specs=(vmem, vmem),
        scratch_shapes=[
            pltpu.VMEM((2, 4, 2, 4, rows, width), bf16),
            pltpu.VMEM((width, depth), bf16),
            pltpu.VMEM((width, depth), bf16),
            pltpu.VMEM((4, 4, 8, count), f32),
            pltpu.VMEM((4, 4, count, count), f32),
            dma((2,)),
            dma((80,)),
            dma((2, 4, 4)),
            dma((2, 2)),
            dma((2, 4, 4)),
            dma((4, 4)),
        ],
        compiler_params=pltpu.CompilerParams(
            collective_id=0, has_side_effects=True, vmem_limit_bytes=VMEM_LIMIT
        ),
        name="gather",
    )(tokens, meta, w_gate[0], w_up[0])

    mixed = pl.pallas_call(
        scatter_kernel,
        out_shape=jax.ShapeDtypeStruct((2, 4, rows // 2, width), bf16),
        in_specs=[vmem, hbm],
        out_specs=hbm,
        scratch_shapes=[
            pltpu.VMEM((depth, width), bf16),
            pltpu.VMEM((2, 4, 4, rows, width), bf16),
            pltpu.VMEM((2, 4, 4, rows, width), bf16),
            pltpu.VMEM((2, 4, 4, rows, width), bf16),
            pltpu.VMEM((2, 2, 2, rows, width), bf16),
            pltpu.VMEM((2, 2, 4, rows, width), bf16),
            pltpu.VMEM((2, 4, rows, width), bf16),
            pltpu.VMEM((2, 2, rows // 2, width), bf16),
            pltpu.VMEM((2, 2, rows, width), bf16),
            pltpu.VMEM((4, rows // 2, width), bf16),
            pltpu.VMEM((3, rows // 2, width), bf16),
            pltpu.VMEM((2, 4, rows // 2, width), bf16),
            dma(()),
            dma((64,)),
            dma((2, 4)),
            dma((2, 2, 2)),
            dma((2, 2, 4)),
            dma((2, 2)),
            dma((2, 2)),
            dma((3,)),
            dma((3,)),
            dma((4,)),
            dma(()),
        ],
        compiler_params=pltpu.CompilerParams(
            collective_id=1, has_side_effects=True, vmem_limit_bytes=VMEM_LIMIT
        ),
        name="scatter",
    )(hidden, w_down[0])
    return (mixed.reshape(count, width), loads[:, 0])


def solution(mesh):
    torus = Mesh(mesh.devices.reshape(4, 4, 4, 2), DP + EXPERT)
    in_specs = (
        P(DP, None),
        P(DP, None),
        P(DP, None),
        P(DP),
        P(EXPERT, None, DP),
        P(EXPERT, None, DP),
        P(EXPERT, DP, None),
    )
    out_specs = (P(DP, None), P())
    return jax.shard_map(
        per_device, mesh=torus, in_specs=in_specs, out_specs=out_specs, check_vma=False
    )
```

time: 303 us -> 155 us (0.51)
  waiting for transfers between devices: 190 us -> 0 us
  Pallas kernels: 0 us -> 148 us
  matrix products: 35.1 us -> 0 us
  blocking collectives: 32.7 us -> 0 us
  between operations: 14.8 us -> 1.3 us
  local copies, waits for them, and re-layouts: 14.1 us -> 3.59 us
  other arithmetic: 10.5 us -> 1.3 us
  starting transfers between devices: 4.58 us -> 0 us
    pallas_call x0 -> x2, Pallas kernels: none -> 148 us  [the longest x1 79.7 us: per_device(): pl.pallas_call(scatter_kernel, out_shape=jax.ShapeDtypeStruct((2, 4, rows...]
    reduce_scatter x1 -> x0, waiting for transfers between devices: 94.7 us -> none  [per_device(): lax.psum_scatter(jnp.dot(hidden, down_matrix, preferred_element_type=jnp....]
    all_gather x1 -> x0, waiting for transfers between devices: 93.1 us -> none  [per_device(): gathered = lax.all_gather(outbound, DP, axis=0, tiled=True)]
    dot_general x3 -> x0, matrix products: 35.1 us -> none  [the longest x1 21.9 us: per_device(): jnp.dot(hidden, down_matrix, preferred_element_type=jnp.float32)]
    all_to_all x1 -> x0, blocking collectives: 20.2 us -> none  [sum_at_owner(): tiles = lax.all_to_all(split_up(shard, dim, size), axis, 0, 0, tiled=True)]
    psum x2 -> x0, blocking collectives: 12.6 us -> none  [over_axes(): shard = lax.psum(shard, axis)]
    reduce_sum x3 -> x1, other arithmetic: 8.96 us -> 1.3 us  [per_device(): meta = jnp.sum(jnp.where(named, gates[:, None, :], 0.0), axis=0)]
    gather x1 -> x0, local copies, waits for them, and re-layouts: 5.12 us -> none  [per_device(): selected = summed[pick_index].astype(jnp.float32)]
  transfers between devices with their start and end apart: 3 -> 0, of which waited for: 3 -> 0; matrix products, arithmetic and copies ran while one was open for 0% -> 0% of each run, Pallas kernels for 0% -> 0%
where the time goes in v1:
time: 155 us; the launch traced here: 154 us
  Pallas kernels  148 us (95%)
  local copies, waits for them, and re-layouts  3.59 us (2%)
    pallas_call x1, Pallas kernels, per_device(): pl.pallas_call(scatter_kernel, out_shape=jax.ShapeDtypeStruct((2, 4, rows...  79.7 us
    pallas_call x1, Pallas kernels, per_device(): pl.pallas_call(gather_kernel, out_shape=(jax.ShapeDtypeStruct((2, 4, 8 *...  68.4 us

profile of v1, /device:TPU:1, one launch (start us, length us, event | category | flops | bytes accessed | tf_op | source)
XLA Modules:
  0.0 154.3 jit_solution(6011326404756944537)
XLA Ops:
  1.3 1.3 select_reduce_fusion.meta
  2.6 68.4 %gather.1 = (bf16[2,4,256,512]{3,2,1,0:T(8,128)(2,1)}, s32[8,128]{1,0:T(8,128)}) custom-call(bf16[128,4096]{1,0:T(8,128)(2,1)} %tok.1, f32[8,128]{1,0:T(8,128)} %select_reduce_fusion.meta, bf16[4096,512]{1,0:T(8,128)(2,1)} %bitcast.10, bf16[4096,512]{1,0:T(8,128)(2,1)} %bitcast.11), custom_call_target="tpu_custom_call" | custom-call | tf_op jit(solution)/shard_map/gather/pallas_call | solution.py:341
  71.0 79.7 %scatter.1 = bf16[2,4,16,4096]{3,2,1,0:T(8,128)(2,1)} custom-call(bf16[2,4,256,512]{3,2,1,0:T(8,128)(2,1)} %get-tuple-element.4.hid, bf16[512,4096]{1,0:T(8,128)(2,1)} %bitcast.8), custom_call_target="tpu_custom_call" | custom-call | tf_op jit(solution)/shard_map/scatter/pallas_call | solution.py:365
  150.7 1.3 slice_reduce_fusion
  152.0 2.3 %copy.11 = bf16[128,4096]{1,0:T(8,128)(2,1)} copy(bf16[128,4096]{1,0:T(8,128)(2,1)} %bitcast.9) | data formatting | bytes 2097152
  (1 shorter events, 0.0 us)

commit v2 on v1

v2 whole, which is shorter than its diff:
```python
import functools
import jax
import jax.numpy as jnp
from jax import lax
from jax.experimental import pallas as pl
from jax.experimental.pallas import tpu as pltpu
from jax.sharding import Mesh
from jax.sharding import PartitionSpec as P

MESH = pl.DeviceIdType.MESH
DP = ("z", "y")
EXPERT = ("x", "c")
RINGS = (("y", "z"), ("z", "y"))
ORDERS = (("z", "x", "y"), ("y", "z", "x"), ("x", "y", "z"))
LANES = 128
BY_X = 10
PARTS = (12, 12, 8)
VMEM_LIMIT = 67043328


def shifted(axis, by):
    return lax.rem(lax.axis_index(axis) + by % 4, 4)


def other_core():
    return {"c": 1 - lax.axis_index("c")}


class Sender:
    def __init__(self, sems):
        self.sems, self.copies = sems, []

    def __call__(self, src, dst, recv_sem, where):
        copy = pltpu.make_async_remote_copy(
            src_ref=src,
            dst_ref=dst,
            send_sem=self.sems.at[len(self.copies)],
            recv_sem=recv_sem,
            device_id=where,
            device_id_type=MESH,
        )
        copy.start()
        self.copies.append(copy)

    def drain(self):
        for copy in self.copies:
            copy.wait_send()


def landed(ref, sem):
    pltpu.make_async_copy(ref, ref, sem).wait()


def enter(peers):
    barrier = pltpu.get_barrier_semaphore()
    for peer in peers:
        pl.semaphore_signal(barrier, inc=1, device_id=peer, device_id_type=MESH)
    pl.semaphore_wait(barrier, len(peers))


def gather_kernel(
    tok, meta, wg_hbm, wu_hbm, hid, loads, x, wg, wu, m, wcol,
    wsem, send_sem, blk_sem, half_sem, side_sem, swap_sem, meta_sem,
):
    c, xi = lax.axis_index("c"), lax.axis_index("x")
    expert = xi * 2 + c
    parity = lax.rem(xi, 2)
    loads_in = [pltpu.make_async_copy(wg_hbm, wg, wsem.at[0]), pltpu.make_async_copy(wu_hbm, wu, wsem.at[1])]
    for copy in loads_in:
        copy.start()
    rows, width = x.shape[4], x.shape[5]
    half = rows // 2
    by_x = BY_X * LANES
    by_plane = width - by_x
    mine = pl.ds(pl.multiple_of(parity * by_x, LANES), by_plane)
    given = pl.ds(pl.multiple_of(parity * by_plane, LANES), by_x)
    taken = pl.ds(pl.multiple_of((1 - parity) * by_plane, LANES), by_x)
    peers = [(i, j) for i in range(4) for j in range(4) if (i, j) != (0, 0)]
    enter(
        [other_core()]
        + [{"x": shifted("x", 1)}, {"x": shifted("x", -1)}]
        + [{"z": shifted("z", i), "y": shifted("y", j)} for i, j in peers]
    )
    send = Sender(send_sem)

    def own_rows(h, o):
        owner = c if o == 0 else 1 - c
        return pl.ds(pl.multiple_of(owner * (2 * rows) + h * rows, rows), rows)

    for h in range(2):
        own = tok.at[own_rows(h, 0), mine]
        a1, a2 = RINGS[h]
        send(own, x.at[h, 0, 3, 0, :, mine], blk_sem.at[h, 0, 3], {a1: shifted(a1, 1)})
        send(own, x.at[h, 0, 1, 0, :, mine], blk_sem.at[h, 0, 1], {a1: shifted(a1, -1)})
    for h in range(2):
        own = tok.at[own_rows(h, 0), mine]
        a1, a2 = RINGS[h]
        send(own, x.at[h, 3, 0, 0, :, mine], blk_sem.at[h, 3, 0], {a2: shifted(a2, 1)})
        send(own, x.at[h, 1, 0, 0, :, mine], blk_sem.at[h, 1, 0], {a2: shifted(a2, -1)})
    for i, j in peers:
        at = (-i % 4, -j % 4)
        send(meta, m.at[at], meta_sem.at[at], {"z": shifted("z", i), "y": shifted("y", j)})
    m[0, 0] = meta[...]
    for h in range(2):
        for o in range(2):
            x[h, 0, 0, o] = tok[own_rows(h, o), :]

    def aside(h, g, b):
        step = 1 if (b // 2 + g // 2 + h) % 2 == 0 else -1
        part = x.at[h, g, b, 0, :, given]
        send(part, part, side_sem.at[h, g, b], {"x": shifted("x", step)})

    def swap(h, g, b):
        landed(x.at[h, g, b, 0, :, taken], side_sem.at[h, g, b])
        send(x.at[h, g, b, 0], x.at[h, g, b, 1], swap_sem.at[h, g, b], other_core())

    def spread(h, b):
        a2 = RINGS[h][1]
        part = x.at[h, 0, b, 0, :, mine]
        send(part, x.at[h, 3, b, 0, :, mine], blk_sem.at[h, 3, b], {a2: shifted(a2, 1)})
        send(part, x.at[h, 1, b, 0, :, mine], blk_sem.at[h, 1, b], {a2: shifted(a2, -1)})
        aside(h, 0, b)

    def near(h):
        a1 = RINGS[h][0]
        for b, step, part in ((3, 1, 0), (1, -1, 1)):
            landed(x.at[h, 0, b, 0, :, mine], blk_sem.at[h, 0, b])
            piece = pl.ds(part * half, half)
            send(
                x.at[h, 0, b, 0, piece, mine],
                x.at[h, 0, 2, 0, piece, mine],
                half_sem.at[h, part],
                {a1: shifted(a1, step)},
            )
        for b in (3, 1):
            spread(h, b)

    def far(h):
        for part in range(2):
            landed(x.at[h, 0, 2, 0, pl.ds(part * half, half), mine], half_sem.at[h, part])
        spread(h, 2)

    def onward(h, b):
        a2 = RINGS[h][1]
        for g, step, passes in ((3, 1, (0, 2)), (1, -1, (3, 1))):
            part = x.at[h, g, b, 0, :, mine]
            landed(part, blk_sem.at[h, g, b])
            if b in passes:
                send(part, x.at[h, 2, b, 0, :, mine], blk_sem.at[h, 2, b], {a2: shifted(a2, step)})
            aside(h, g, b)

    def last(h, b):
        landed(x.at[h, 2, b, 0, :, mine], blk_sem.at[h, 2, b])
        aside(h, 2, b)

    def weigh():
        for i, j in peers:
            landed(m.at[i, j], meta_sem.at[i, j])
        total = jnp.zeros(m.shape[2:], jnp.float32)
        for i in range(4):
            for j in range(4):
                total = total + jnp.where(m[i, j] > 0.0, 1.0, 0.0)
                row = m[i, j, pl.ds(expert, 1), :]
                wcol[i, j] = jnp.transpose(jnp.broadcast_to(row, (row.shape[1], row.shape[1])))
        loads[...] = jnp.broadcast_to(jnp.sum(total, axis=1, keepdims=True), loads.shape).astype(jnp.int32)

    def compute(blocks):
        places, parts = [], []
        for h, g, b in blocks:
            if (g, b) != (0, 0):
                landed(x.at[h, g, b, 1], swap_sem.at[h, g, b])
            at = (g, b) if h == 0 else (b, g)
            for o in range(2):
                parts.append(wcol[at[0], at[1], own_rows(h, o), :])
                for k in range(2):
                    places.append((*at, lax.rem(2 * h + k + 4 - xi, 4), o))
        weight = jnp.concatenate(parts, axis=0)
        weight = jnp.concatenate([weight, weight], axis=1)

        @pl.loop(0, 2)
        def _(n):
            cols = pl.ds(pl.multiple_of(n * 256, 256), 256)
            lhs = jnp.concatenate([x[block].reshape(2 * rows, width) for block in blocks], axis=0)
            gate = jnp.dot(lhs, wg[:, cols], preferred_element_type=jnp.float32)
            up = jnp.dot(lhs, wu[:, cols], preferred_element_type=jnp.float32)
            act = (gate / (1.0 + jnp.exp(-gate)) * up * weight).astype(jnp.bfloat16)
            for k, place in enumerate(places):
                hid[(*place, slice(None), cols)] = act[k * half : (k + 1) * half]

    both = lambda g, b: [(0, g, b), (1, g, b)]
    near(0), near(1)
    far(0), far(1)
    onward(0, 0), onward(1, 0)
    weigh()
    for copy in loads_in:
        copy.wait()
    swap(0, 0, 3), swap(1, 0, 3), swap(0, 0, 1), swap(1, 0, 1)
    onward(0, 3), onward(1, 3)
    swap(0, 0, 2), swap(1, 0, 2)
    compute(both(0, 3) + both(0, 1))
    for h in range(2):
        swap(h, 3, 0), swap(h, 1, 0)
    onward(0, 1), onward(1, 1)
    compute(both(0, 0) + both(0, 2))
    last(0, 0), last(1, 0)
    for h in range(2):
        swap(h, 3, 3), swap(h, 1, 3)
    compute(both(3, 0) + both(1, 0))
    onward(0, 2), onward(1, 2)
    last(0, 3), last(1, 3)
    for h in range(2):
        swap(h, 3, 1), swap(h, 1, 1)
    compute(both(3, 3) + both(1, 3))
    last(0, 1), last(1, 1)
    swap(0, 2, 0), swap(1, 2, 0)
    for h in range(2):
        swap(h, 3, 2), swap(h, 1, 2)
    compute(both(3, 1) + both(1, 1))
    last(0, 2), last(1, 2)
    swap(0, 2, 3), swap(1, 2, 3)
    swap(0, 2, 1), swap(1, 2, 1)
    compute(both(3, 2) + both(1, 2))
    swap(0, 2, 2), swap(1, 2, 2)
    compute(both(2, 0) + both(2, 3))
    compute(both(2, 1) + both(2, 2))
    send.drain()


WAYS = ((1, 1, (2, 0)), (-1, 3, (1, 3)))


class Level:
    def __init__(self, send, axis, src, far, near, far_sem, near_sem):
        self.send, self.axis, self.src = send, axis, src
        self.far, self.near, self.far_sem, self.near_sem = far, near, far_sem, near_sem

    def send_far(self):
        for k in range(2):
            for way, (step, _, blocks) in enumerate(WAYS):
                self.send(
                    self.src(2, blocks[k]), self.far(way, k), self.far_sem.at[way, k], {self.axis: shifted(self.axis, step)}
                )

    def send_near(self, way, b):
        step, g, _ = WAYS[way]
        self.send(self.src(g, b), self.near(way, b), self.near_sem.at[way, b], {self.axis: shifted(self.axis, step)})

    def send_direct(self, way):
        for b in (2, 1, 3, 0):
            if b not in WAYS[way][2]:
                self.send_near(way, b)

    def pass_on(self, k):
        for way, (_, g, blocks) in enumerate(WAYS):
            landed(self.far(way, k), self.far_sem.at[way, k])
            add_up(self.src(g, blocks[k]), [self.src(g, blocks[k]), self.far(way, k)])
            self.send_near(way, blocks[k])

    def collect(self, b, out):
        for way in range(2):
            landed(self.near(way, b), self.near_sem.at[way, b])
        add_up(out, [self.src(0, b), self.near(0, b), self.near(1, b)])


def add_up(out, terms):
    total = terms[0][...].astype(jnp.float32)
    for term in terms[1:]:
        total = total + term[...].astype(jnp.float32)
    out[...] = total.astype(jnp.bfloat16)


def scatter_kernel(
    hid, wd_hbm, out, wd, s, p, l, f1, n1, t, f2, n2, u, f3, n3, ob,
    wsem, send_sem, l_sem, f1_sem, n1_sem, f2_sem, n2_sem, f3_sem, n3_sem, ox_sem, od_sem, out_sem,
):
    c, xi = lax.axis_index("c"), lax.axis_index("x")
    load = pltpu.make_async_copy(wd_hbm, wd, wsem)
    load.start()
    enter([other_core()] + [{a: shifted(a, by)} for a in ("x", "y", "z") for by in (1, -1)] + [{"x": shifted("x", 2)}])
    send = Sender(send_sem)
    load.wait()
    every = range(3)
    sizes = [n * LANES for n in PARTS]
    starts = [sum(sizes[:q]) for q in every]
    span = [pl.ds(0, n) for n in sizes]
    first = [
        Level(
            send,
            ORDERS[q][0],
            lambda g, b, q=q: s.at[q, g, b, :, :, span[q]],
            lambda way, k, q=q: f1.at[q, way, k, :, :, span[q]],
            lambda way, b, q=q: n1.at[q, way, b, :, :, span[q]],
            f1_sem.at[q],
            n1_sem.at[q],
        )
        for q in every
    ]
    second = [
        Level(
            send,
            ORDERS[q][1],
            lambda g, b, q=q: t.at[q, g, b, :, span[q]],
            lambda way, k, q=q: f2.at[q, way, k, :, span[q]],
            lambda way, b, q=q: n2.at[q, way, b, :, span[q]],
            f2_sem.at[q],
            n2_sem.at[q],
        )
        for q in every
    ]

    def compute(q, i):
        pieces = []
        for o in range(2):
            for j in range(4):
                for k in range(4):
                    at = dict(zip(ORDERS[q], (i, j, k)))
                    pieces.append((at["z"], at["y"], at["x"], o))
        for lo in range(0, sizes[q], 512):
            n = min(512, sizes[q] - lo)
            lhs = jnp.concatenate([hid[piece] for piece in pieces], axis=0)
            y = jnp.dot(lhs, wd[:, starts[q] + lo : starts[q] + lo + n], preferred_element_type=jnp.float32)
            y = y.astype(jnp.bfloat16).reshape(2, 4, 4, lhs.shape[0] // 32, n)
            s[q, i, :, :, :, lo : lo + n] = y[0]
            p[q, i, :, :, :, lo : lo + n] = y[1]
        send(p.at[q, i, :, :, :, span[q]], l.at[q, i, :, :, :, span[q]], l_sem.at[q, i], other_core())

    def chip_sum(q, i):
        landed(l.at[q, i, :, :, :, span[q]], l_sem.at[q, i])

        @pl.loop(0, 4)
        def _(j):
            add_up(s.at[q, i, j, :, :, span[q]], [s.at[q, i, j, :, :, span[q]], l.at[q, i, j, :, :, span[q]]])

    for q in every:
        compute(q, 2)
    for q in every:
        chip_sum(q, 2)
        first[q].send_far()
    for q in every:
        compute(q, 1)
    for q in every:
        chip_sum(q, 1)
        first[q].send_direct(0)
    for q in every:
        compute(q, 3)
    for q in every:
        chip_sum(q, 3)
        first[q].send_direct(1)
    for q in every:
        first[q].pass_on(0)
    for q in every:
        compute(q, 0)
    for q in every:
        first[q].pass_on(1)
    for q in every:
        chip_sum(q, 0)
    down = lambda q, b: first[q].collect(b, t.at[q, b, :, :, span[q]])
    for q in every:
        down(q, 2)
        second[q].send_far()
    for q in every:
        down(q, 1)
        second[q].send_direct(0)
        down(q, 3)
        second[q].send_direct(1)
    for q in every:
        second[q].pass_on(0)
    for q in every:
        down(q, 0)
    for q in every:
        second[q].pass_on(1)
    ends = [u.at[q, :, :, span[q]] for q in every]
    for q in every:
        a = ORDERS[q][2]
        second[q].collect(2, ends[q].at[2])
        send(ends[q].at[2], f3.at[q, :, span[q]], f3_sem.at[q], {a: shifted(a, 1)})
    for q in every:
        a = ORDERS[q][2]
        second[q].collect(3, ends[q].at[3])
        send(ends[q].at[3], n3.at[q, 1, :, span[q]], n3_sem.at[q, 1], {a: shifted(a, -1)})
    for q in every:
        a = ORDERS[q][2]
        second[q].collect(1, ends[q].at[1])
        landed(f3.at[q, :, span[q]], f3_sem.at[q])
        add_up(ends[q].at[1], [ends[q].at[1], f3.at[q, :, span[q]]])
        send(ends[q].at[1], n3.at[q, 0, :, span[q]], n3_sem.at[q, 0], {a: shifted(a, 1)})
    for q in every:
        second[q].collect(0, ends[q].at[0])
    for q in every:
        for way in range(2):
            landed(n3.at[q, way, :, span[q]], n3_sem.at[q, way])
        cols = pl.ds(starts[q], sizes[q])
        done = ob.at[c, xi, :, cols]
        add_up(done, [ends[q].at[0], n3.at[q, 0, :, span[q]], n3.at[q, 1, :, span[q]]])
        for by in (2, 1, 3):
            send(done, done, ox_sem.at[q, by - 1], {"x": shifted("x", by)})
        send(done, done, od_sem.at[q, 0], other_core())
    for q in every:
        cols = pl.ds(starts[q], sizes[q])
        for by in (1, 3, 2):
            part = ob.at[c, lax.rem(xi + 4 - by, 4), :, cols]
            landed(part, ox_sem.at[q, by - 1])
            send(part, part, od_sem.at[q, by], other_core())
    for q in every:
        for by in range(4):
            landed(ob.at[1 - c, lax.rem(xi + 4 - by, 4), :, pl.ds(starts[q], sizes[q])], od_sem.at[q, by])
    store = pltpu.make_async_copy(ob, out, out_sem)
    store.start()
    store.wait()
    send.drain()


def per_device(tokens, expert_ids, gate_weights, live_counts, w_gate, w_up, w_down):
    count, width = tokens.shape
    depth = w_gate.shape[2]
    rows = count // 4
    half = rows // 2
    dma = pltpu.SemaphoreType.DMA
    bf16, f32 = jnp.bfloat16, jnp.float32
    is_live = jnp.arange(count, dtype=jnp.int32)[None, :] < live_counts[0]
    ids, gates = expert_ids.T, gate_weights.T
    named = (ids[:, None, :] == jnp.arange(8, dtype=jnp.int32)[None, :, None]) & is_live[None]
    meta = jnp.sum(jnp.where(named, gates[:, None, :], 0.0), axis=0)

    vmem = pl.BlockSpec(memory_space=pltpu.VMEM)
    hbm = pl.BlockSpec(memory_space=pl.ANY)
    hidden, loads = pl.pallas_call(
        gather_kernel,
        out_shape=(
            jax.ShapeDtypeStruct((4, 4, 4, 2, half, depth), bf16),
            jax.ShapeDtypeStruct((8, 128), jnp.int32),
        ),
        in_specs=[vmem, vmem, hbm, hbm],
        out_specs=(vmem, vmem),
        scratch_shapes=[
            pltpu.VMEM((2, 4, 4, 2, rows, width), bf16),
            pltpu.VMEM((width, depth), bf16),
            pltpu.VMEM((width, depth), bf16),
            pltpu.VMEM((4, 4, 8, count), f32),
            pltpu.VMEM((4, 4, count, count), f32),
            dma((2,)),
            dma((112,)),
            dma((2, 4, 4)),
            dma((2, 2)),
            dma((2, 4, 4)),
            dma((2, 4, 4)),
            dma((4, 4)),
        ],
        compiler_params=pltpu.CompilerParams(
            collective_id=0, has_side_effects=True, vmem_limit_bytes=VMEM_LIMIT
        ),
        name="gather",
    )(tokens, meta, w_gate[0], w_up[0])

    broad = max(PARTS) * LANES
    block = lambda *dims: pltpu.VMEM((3, *dims, half, broad), bf16)
    mixed = pl.pallas_call(
        scatter_kernel,
        out_shape=jax.ShapeDtypeStruct((2, 4, half, width), bf16),
        in_specs=[vmem, hbm],
        out_specs=hbm,
        scratch_shapes=[
            pltpu.VMEM((depth, width), bf16),
            block(4, 4, 4),
            block(4, 4, 4),
            block(4, 4, 4),
            block(2, 2, 4),
            block(2, 4, 4),
            block(4, 4),
            block(2, 2),
            block(2, 4),
            block(4),
            block(),
            block(2),
            pltpu.VMEM((2, 4, half, width), bf16),
            dma(()),
            dma((128,)),
            dma((3, 4)),
            dma((3, 2, 2)),
            dma((3, 2, 4)),
            dma((3, 2, 2)),
            dma((3, 2, 4)),
            dma((3,)),
            dma((3, 2)),
            dma((3, 3)),
            dma((3, 4)),
            dma(()),
        ],
        compiler_params=pltpu.CompilerParams(
            collective_id=1, has_side_effects=True, vmem_limit_bytes=VMEM_LIMIT
        ),
        name="scatter",
    )(hidden, w_down[0])
    return (mixed.reshape(count, width), loads[:, 0])


def solution(mesh):
    torus = Mesh(mesh.devices.reshape(4, 4, 4, 2), DP + EXPERT)
    in_specs = (
        P(DP, None),
        P(DP, None),
        P(DP, None),
        P(DP),
        P(EXPERT, None, DP),
        P(EXPERT, None, DP),
        P(EXPERT, DP, None),
    )
    out_specs = (P(DP, None), P())
    return jax.shard_map(
        per_device, mesh=torus, in_specs=in_specs, out_specs=out_specs, check_vma=False
    )
```

time: 155 us -> 132 us (0.85)
  Pallas kernels: 148 us -> 126 us
    pallas_call x2, Pallas kernels: 148 us -> 126 us  [the longest x1 64.6 us: per_device(): pl.pallas_call(gather_kernel, out_shape=(jax.ShapeDtypeStruct((4, 4, 4, 2...]
where the time goes in v2:
time: 132 us
  Pallas kernels  126 us (95%)
  local copies, waits for them, and re-layouts  3.59 us (3%)
    pallas_call x1, Pallas kernels, per_device(): pl.pallas_call(gather_kernel, out_shape=(jax.ShapeDtypeStruct((4, 4, 4, 2...  64.6 us
    pallas_call x1, Pallas kernels, per_device(): pl.pallas_call(scatter_kernel, out_shape=jax.ShapeDtypeStruct((2, 4, half...  61.2 us

profile of v2, /device:TPU:1, one launch (start us, length us, event | category | flops | bytes accessed | tf_op | source)
XLA Modules:
  0.0 132.1 jit_solution(2316469304168561696)
XLA Ops:
  1.3 1.3 select_reduce_fusion.meta
  2.6 64.6 %gather.1 = (bf16[4,4,4,2,16,512]{5,4,3,2,1,0:T(8,128)(2,1)}, s32[8,128]{1,0:T(8,128)}) custom-call(bf16[128,4096]{1,0:T(8,128)(2,1)} %tok.1, f32[8,128]{1,0:T(8,128)} %select_reduce_fusion.meta, bf16[4096,512]{1,0:T(8,128)(2,1)} %bitcast.10, bf16[4096,512]{1,0:T(8,128)(2,1)} %bitcast.11), custom_call_target="tpu_custom_call" | custom-call | tf_op jit(solution)/shard_map/gather/pallas_call | solution.py:427
  67.2 61.2 %scatter.1 = bf16[2,4,16,4096]{3,2,1,0:T(8,128)(2,1)} custom-call(bf16[4,4,4,2,16,512]{5,4,3,2,1,0:T(8,128)(2,1)} %get-tuple-element.4.hid, bf16[512,4096]{1,0:T(8,128)(2,1)} %bitcast.8), custom_call_target="tpu_custom_call" | custom-call | tf_op jit(solution)/shard_map/scatter/pallas_call | solution.py:457
  128.5 1.3 slice_reduce_fusion
  129.8 2.3 %copy.11 = bf16[128,4096]{1,0:T(8,128)(2,1)} copy(bf16[128,4096]{1,0:T(8,128)(2,1)} %bitcast.9) | data formatting | bytes 2097152
  (1 shorter events, 0.0 us)

commit v3 on v0

v3 whole, which is shorter than its diff:
```python
import functools
import math
import jax
import jax.numpy as jnp
from jax import lax
from jax.experimental import pallas as pl
from jax.experimental.pallas import tpu as pltpu
from jax.sharding import Mesh
from jax.sharding import PartitionSpec as P

MESH = pl.DeviceIdType.MESH
DP = ("z", "y")
EXPERT = ("x", "c")
RINGS = (("y", "z"), ("z", "y"))
ORDERS = (("z", "x", "y"), ("y", "z", "x"), ("x", "y", "z"))
LANES = 128
BY_X = 12
PARTS = (12, 12, 8)
STREAMS = 2
VMEM_LIMIT = 67043328


def shifted(axis, by):
    return lax.rem(lax.axis_index(axis) + by % 4, 4)


def other_core():
    return {"c": 1 - lax.axis_index("c")}


class Sender:
    def __init__(self, sem):
        self.sem, self.size = sem, 0

    def __call__(self, src, dst, recv_sem, where):
        self.size += math.prod(src.shape)
        pltpu.make_async_remote_copy(
            src_ref=src, dst_ref=dst, send_sem=self.sem, recv_sem=recv_sem, device_id=where, device_id_type=MESH
        ).start()

    def drain(self, alike):
        assert math.prod(alike.shape) == self.size
        landed(alike, self.sem)


def landed(ref, sem):
    pltpu.make_async_copy(ref, ref, sem).wait()


def enter(peers):
    barrier = pltpu.get_barrier_semaphore()
    for peer in peers:
        pl.semaphore_signal(barrier, inc=1, device_id=peer, device_id_type=MESH)
    pl.semaphore_wait(barrier, len(peers))


class Gather:
    def __init__(self, send, tok, x, base, sems):
        self.send, self.tok, self.x, self.base = send, tok, x, base
        self.near_sem, self.half_sem, self.on_sem, self.side0_sem, self.side_sem, self.last_sem, self.swap_sem = sems
        self.rows, self.width = x.shape[4], x.shape[5]
        parity = lax.rem(lax.axis_index("x"), 2)
        by_x = BY_X * LANES
        by_plane = self.width - by_x
        at = lambda place, size: pl.ds(pl.multiple_of(place, LANES), size)
        self.mine = at(parity * by_x, by_plane)
        self.halves = [at(parity * by_x + n * (by_plane // 2), by_plane // 2) for n in range(2)]
        self.given = at(parity * by_plane, by_x)
        self.taken = at((1 - parity) * by_plane, by_x)

    def own_rows(self, h, o):
        c = lax.axis_index("c")
        owner = c if o == 0 else 1 - c
        start = owner * (self.tok.shape[0] // 2) + self.base + h * self.rows
        return pl.ds(pl.multiple_of(start, self.rows), self.rows)

    def start(self):
        for ring in range(2):
            for h in range(2):
                own = self.tok.at[self.own_rows(h, 0), self.mine]
                a = RINGS[h][ring]
                for step, off in ((1, 3), (-1, 1)):
                    g, b = (0, off) if ring == 0 else (off, 0)
                    to = self.x.at[h, g, b, 0, :, self.mine]
                    sem = self.near_sem.at[h] if ring == 0 else self.on_sem.at[h, 0]
                    self.send(own, to, sem, {a: shifted(a, step)})

    def fill(self):
        for h in range(2):
            for o in range(2):
                self.x[h, 0, 0, o] = self.tok[self.own_rows(h, o), :]

    def aside(self, h, g, b):
        step = 1 if (b // 2 + g // 2 + h) % 2 == 0 else -1
        part = self.x.at[h, g, b, 0, :, self.given]
        sem = self.side0_sem.at[h, int(b == 2)] if g == 0 else self.side_sem.at[h, b]
        self.send(part, part, sem, {"x": shifted("x", step)})

    def swap(self, h, g, b):
        chunk = [(g, b) in pairs for pairs in CHUNKS].index(True)
        self.send(self.x.at[h, g, b, 0], self.x.at[h, g, b, 1], self.swap_sem.at[chunk], other_core())

    passes = {3: (1, (0, 2)), 1: (-1, (3, 1))}

    def forward(self, h, g, b, cols):
        step, blocks = self.passes[g]
        if b in blocks:
            a2 = RINGS[h][1]
            to = self.x.at[h, 2, b, 0, :, cols]
            self.send(self.x.at[h, g, b, 0, :, cols], to, self.last_sem.at[h, b], {a2: shifted(a2, step)})

    def joined_near(self, h):
        landed(self.x.at[h, 0, pl.ds(0, 2), 0, :, self.taken], self.side0_sem.at[h, 0])
        self.swap(h, 0, 3)
        self.swap(h, 0, 1)

    def joined_far(self, h):
        landed(self.x.at[h, 0, 2, 0, :, self.taken], self.side0_sem.at[h, 1])
        self.swap(h, 0, 2)

    def joined(self, h, b):
        landed(self.x.at[h, pl.ds(0, 2), b, 0, :, self.taken], self.side_sem.at[h, b])
        for g in (3, 1):
            self.forward(h, g, b, self.taken)
        for g in (3, 1):
            self.swap(h, g, b)

    def spread(self, h, b):
        a2 = RINGS[h][1]
        for step, g in ((1, 3), (-1, 1)):
            to = self.x.at[h, g, b, 0, :, self.mine]
            self.send(self.x.at[h, 0, b, 0, :, self.mine], to, self.on_sem.at[h, b], {a2: shifted(a2, step)})
        self.aside(h, 0, b)

    def near(self, h):
        a1 = RINGS[h][0]
        landed(self.x.at[h, 0, pl.ds(0, 2), 0, :, self.mine], self.near_sem.at[h])
        for b, step, part in ((3, 1, 0), (1, -1, 1)):
            cols = self.halves[part]
            to = self.x.at[h, 0, 2, 0, :, cols]
            self.send(self.x.at[h, 0, b, 0, :, cols], to, self.half_sem.at[h], {a1: shifted(a1, step)})
        for b in (3, 1):
            self.spread(h, b)

    def far(self, h):
        landed(self.x.at[h, 0, 2, 0, :, self.mine], self.half_sem.at[h])
        self.spread(h, 2)

    def onward(self, h, b):
        landed(self.x.at[h, pl.ds(0, 2), b, 0, :, self.mine], self.on_sem.at[h, b])
        for g in (3, 1):
            self.forward(h, g, b, self.mine)
        for g in (3, 1):
            self.aside(h, g, b)

    def last(self, h, b):
        landed(self.x.at[h, 2, b, 0], self.last_sem.at[h, b])
        self.swap(h, 2, b)

    def compute(self, chunk, wg, wu, wcol, hid):
        pairs = CHUNKS[chunk]
        blocks = [(h, g, b) for g, b in pairs for h in range(2)]
        places, parts = [], []
        count = sum(block[1:] != (0, 0) for block in blocks)
        wide = 4 if count % 4 == 0 else 2
        landed(self.x.at[0, pl.ds(0, count // wide), pl.ds(0, wide), 0], self.swap_sem.at[chunk])
        for h, g, b in blocks:
            at = (g, b) if h == 0 else (b, g)
            for o in range(2):
                parts.append(wcol[at[0], at[1], self.own_rows(h, o), :])
                places.append((*at, o, pl.ds(h * self.rows, self.rows)))
        weight = jnp.concatenate(parts, axis=0)
        weight = jnp.concatenate([weight, weight], axis=1)
        rows = self.rows

        @pl.loop(0, 2)
        def _(n):
            cols = pl.ds(pl.multiple_of(n * 256, 256), 256)
            lhs = jnp.concatenate([self.x[block].reshape(2 * rows, self.width) for block in blocks], axis=0)
            gate = jnp.dot(lhs, wg[:, cols], preferred_element_type=jnp.float32)
            up = jnp.dot(lhs, wu[:, cols], preferred_element_type=jnp.float32)
            act = (gate / (1.0 + jnp.exp(-gate)) * up * weight).astype(jnp.bfloat16)
            for k, place in enumerate(places):
                hid[(*place, cols)] = act[k * rows : (k + 1) * rows]


def pass_meta(m, send, sems, stage):
    if stage == 0:
        send(m.at[0, 0], m.at[0, 3], sems.at[0], {"y": shifted("y", 1)})
        send(m.at[0, 0], m.at[0, 1], sems.at[0], {"y": shifted("y", -1)})
    elif stage == 1:
        landed(m.at[0, pl.ds(0, 2)], sems.at[0])
        send(m.at[0, 3], m.at[0, 2], sems.at[1], {"y": shifted("y", 1)})
    elif stage == 2:
        landed(m.at[0, 2], sems.at[1])
        send(m.at[0], m.at[3], sems.at[2], {"z": shifted("z", 1)})
        send(m.at[0], m.at[1], sems.at[2], {"z": shifted("z", -1)})
    else:
        landed(m.at[pl.ds(0, 2)], sems.at[2])
        send(m.at[3], m.at[2], sems.at[3], {"z": shifted("z", 1)})


def weigh(m, sems, wcol, loads):
    expert = lax.axis_index("x") * 2 + lax.axis_index("c")
    landed(m.at[2], sems.at[3])
    total = jnp.zeros(m.shape[2:], jnp.float32)
    for i in range(4):
        for j in range(4):
            total = total + jnp.where(m[i, j] > 0.0, 1.0, 0.0)
            row = m[i, j, pl.ds(expert, 1), :]
            wcol[i, j] = jnp.transpose(jnp.broadcast_to(row, (row.shape[1], row.shape[1])))
    counts = jnp.broadcast_to(jnp.sum(total, axis=1, keepdims=True), total.shape)
    place = lax.broadcasted_iota(jnp.int32, total.shape, 0) == lax.broadcasted_iota(jnp.int32, total.shape, 1)
    loads[...] = jnp.sum(jnp.where(place, counts, 0.0), axis=0, keepdims=True).astype(jnp.int32)


WAYS = ((1, 1, (2, 0)), (-1, 3, (1, 3)))


class Level:
    def __init__(self, send, axis, src, far, near, far_sem, near_sem):
        self.send, self.axis, self.src = send, axis, src
        self.far, self.near, self.far_sem, self.near_sem = far, near, far_sem, near_sem

    def to(self, step):
        return {self.axis: shifted(self.axis, step)}

    def send_far(self):
        for k in range(2):
            for way, (step, _, blocks) in enumerate(WAYS):
                self.send(self.src(2, blocks[k]), self.far.at[way, k], self.far_sem.at[k], self.to(step))

    def send_near(self, way, b):
        step, g, _ = WAYS[way]
        self.send(self.src(g, b), self.near.at[way, b], self.near_sem.at[b], self.to(step))

    def send_direct(self, way):
        for b in (2, 1, 3, 0):
            if b not in WAYS[way][2]:
                self.send_near(way, b)

    def pass_on(self, k):
        landed(self.far.at[:, k], self.far_sem.at[k])
        for way, (_, g, blocks) in enumerate(WAYS):
            add_up(self.src(g, blocks[k]), [self.src(g, blocks[k]), self.far.at[way, k]])
            self.send_near(way, blocks[k])

    def collect(self, b, out):
        landed(self.near.at[:, b], self.near_sem.at[b])
        add_up(out, [self.src(0, b), self.near.at[0, b], self.near.at[1, b]])


def add_up(out, terms):
    total = terms[0][...].astype(jnp.float32)
    for term in terms[1:]:
        total = total + term[...].astype(jnp.float32)
    out[...] = total.astype(jnp.bfloat16)


SIZES = [n * LANES for n in PARTS]
STARTS = [sum(SIZES[:q]) for q in range(3)]
QUARTERS = [n // 4 for n in SIZES]


class Scatter:
    def __init__(self, sends, hid, wd, x, s, ob, bufs, sems):
        self.sends = [Sender(sends.at[n]) for n in range(3)]
        swap, first, send = self.sends
        self.swap, self.send, self.hid, self.wd, self.x, self.s, self.ob = swap, send, hid, wd, x, s, ob
        self.rows = s.shape[2]
        self.sems = sems
        self.first, self.second, self.bufs = [], [], bufs
        for q in range(3):
            f1, n1, t, f2, n2, u, f3, n3 = bufs[q]
            self.first.append(
                Level(first, ORDERS[q][0], functools.partial(self.block, q), f1, n1, sems["f1"].at[q], sems["n1"].at[q])
            )
            if q == 1:
                src = lambda g, b, t=t: t.at[g, :, pl.ds(b * QUARTERS[1], QUARTERS[1])]
            else:
                src = lambda g, b, t=t: t.at[g, b]
            self.second.append(Level(send, ORDERS[q][1], src, f2, n2, sems["f2"].at[q], sems["n2"].at[q]))

    def cols(self, q, dx):
        return pl.ds(STARTS[q] + dx * QUARTERS[q], QUARTERS[q])

    def block(self, q, g, b):
        if q == 0:
            return self.s.at[g, :, :, self.cols(0, b)]
        if q == 1:
            return self.s.at[b, g, :, pl.ds(STARTS[1], SIZES[1])]
        return self.s.at[:, b, :, self.cols(2, g)]

    def group(self, ref, q, i):
        if q == 0:
            return ref.at[i, :, :, :, pl.ds(STARTS[0], SIZES[0])]
        if q == 1:
            return ref.at[:, i, :, :, pl.ds(STARTS[1], SIZES[1])]
        return ref.at[:, :, :, :, self.cols(2, i)]

    def ranks(self, q, i):
        every = range(4)
        if q == 0:
            return [(i, j) for j in every]
        if q == 1:
            return [(j, i) for j in every]
        return [(j, k) for j in every for k in every]

    def put(self, y, o, at, cols):
        y = y.astype(jnp.bfloat16)
        if o == 0:
            self.s[(*at, slice(None), cols)] = y
        else:
            self.x[(0, *at, slice(None), slice(None), cols)] = y.reshape(2, self.rows // 2, y.shape[1])

    def compute(self, q, i):
        xi = lax.axis_index("x")
        ranks, rows, size = self.ranks(q, i), self.rows, QUARTERS[q]
        if q == 2:
            quarter = lax.rem(xi + i, 4)
            for o in range(2):
                lhs = jnp.concatenate([self.hid[(*at, o)] for at in ranks], axis=0)
                rhs = self.wd[:, pl.ds(pl.multiple_of(STARTS[2] + quarter * size, LANES), size)]
                y = jnp.dot(lhs, rhs, preferred_element_type=jnp.float32)
                for n, at in enumerate(ranks):
                    self.put(y[n * rows : (n + 1) * rows], o, at, self.cols(2, i))
        else:
            for two in range(2):
                lhs = jnp.concatenate([self.hid[(*at, o)] for o in range(2) for at in ranks], axis=0)
                lo = STARTS[q] + two * 2 * size
                y = jnp.dot(lhs, self.wd[:, lo : lo + 2 * size], preferred_element_type=jnp.float32)
                for k in range(2):
                    place = STARTS[q] + lax.rem(2 * two + k + 4 - xi, 4) * size
                    cols = pl.ds(pl.multiple_of(place, LANES), size)
                    for n in range(8):
                        piece = y[n * rows : (n + 1) * rows, k * size : (k + 1) * size]
                        self.put(piece, n // 4, ranks[n % 4], cols)
        self.swap(self.group(self.x.at[0], q, i), self.group(self.x.at[1], q, i), self.sems["l"].at[q, i], other_core())

    def chip_sum(self, q, i):
        landed(self.group(self.x.at[1], q, i), self.sems["l"].at[q, i])
        cols = self.cols(2, i) if q == 2 else pl.ds(STARTS[q], SIZES[q])
        for at in self.ranks(q, i):
            own = self.s.at[(*at, slice(None), cols)]
            other = self.x[(1, *at, slice(None), slice(None), cols)]
            other = other.reshape(self.rows, other.shape[2])
            own[...] = (own[...].astype(jnp.float32) + other.astype(jnp.float32)).astype(jnp.bfloat16)

    def drain(self):
        width = self.s.shape[3]
        for send, part in zip(self.sends, (width, width // 4 * 3, width // 32 * 11)):
            send.drain(self.s.at[:, :, :, pl.ds(0, part)])

    def down(self, q, b):
        t = self.bufs[q][2]
        self.first[q].collect(b, t.at[b])

    def end(self, q, k):
        a, sems = ORDERS[q][2], self.sems
        u, f3, n3 = self.bufs[q][5:]
        self.second[q].collect(k, u.at[k])
        if k == 2:
            self.send(u.at[2], f3, sems["f3"].at[q], {a: shifted(a, 1)})
        elif k == 3:
            self.send(u.at[3], n3.at[1], sems["n3"].at[q], {a: shifted(a, -1)})
        elif k == 1:
            landed(f3, sems["f3"].at[q])
            add_up(u.at[1], [u.at[1], f3])
            self.send(u.at[1], n3.at[0], sems["n3"].at[q], {a: shifted(a, 1)})

    def piece(self, q, core, chip):
        return self.ob.at[core, :, pl.ds(pl.multiple_of(STARTS[q] + chip * QUARTERS[q], LANES), QUARTERS[q])]

    def share(self, q):
        c, xi = lax.axis_index("c"), lax.axis_index("x")
        u, _, n3 = self.bufs[q][5:]
        landed(n3, self.sems["n3"].at[q])
        done = self.piece(q, c, xi)
        add_up(done, [u.at[0], n3.at[0], n3.at[1]])
        for by in (2, 1, 3):
            self.send(done, done, self.sems["ox"].at[q, by - 1], {"x": shifted("x", by)})
        self.send(done, done, self.sems["od"].at[q], other_core())

    def pair(self, q, by):
        part = self.piece(q, lax.axis_index("c"), lax.rem(lax.axis_index("x") + 4 - by, 4))
        landed(part, self.sems["ox"].at[q, by - 1])
        self.send(part, part, self.sems["od"].at[q], other_core())

    def close(self, q):
        landed(self.ob.at[1 - lax.axis_index("c"), :, pl.ds(STARTS[q], SIZES[q])], self.sems["od"].at[q])


RECV = ("l", "f1", "n1", "f2", "n2", "f3", "n3", "ox", "od")


def moe_kernel(
    tok, meta, wg_hbm, wu_hbm, wd_hbm, ob, loads, x, wg, wu, wd, m, wcol, hid, s, bufs,
    wsem, send_sem, meta_sem, free_sem, collect_sems, recv,
):
    weights = [
        pltpu.make_async_copy(src, dst, wsem.at[n])
        for n, (src, dst) in enumerate(((wg_hbm, wg), (wu_hbm, wu), (wd_hbm, wd)))
    ]
    for copy in weights:
        copy.start()
    m[0, 0] = meta[...]
    enter([other_core(), {"x": shifted("x", 2)}] + [{a: shifted(a, by)} for a in ("x", "y", "z") for by in (1, -1)])
    send = Sender(send_sem.at[0, 0])
    gather, scatter = [], []
    per = tok.shape[0] // 2 // STREAMS
    for n in range(STREAMS):
        gather.append(
            Gather(
                Sender(send_sem.at[n, 1]), tok, x.at[n], n * per, [ref.at[n] for ref in collect_sems]
            )
        )
        sems = {name: ref.at[n] for name, ref in zip(RECV, recv)}
        parts = [tuple(buf.at[n] for buf in part) for part in bufs]
        scatter.append(Scatter(send_sem.at[n, pl.ds(2, 3)], hid.at[n], wd, x.at[n], s.at[n], ob.at[:, n], parts, sems))

    pass_meta(m, send, meta_sem, 0)
    for each in gather:
        each.fill()
    relay = functools.partial(pass_meta, m, send, meta_sem)
    plan(gather, scatter, (wg, wu, wcol), hid, free_sem, weights, relay, lambda: weigh(m, meta_sem, wcol, loads))
    send.drain(wcol.at[0, pl.ds(0, 1), pl.ds(0, 120)])
    for each in scatter:
        each.drain()


ORDER = (
    2000, 1100, 3010, 3000, 5010, 1200, 5000, 4010, 6010, 5013, 8010, 5011, 4000, 5001,
    1300, 5003, 8000, 7010, 6000, 8013, 8011, 2100, 5012, 7000, 5002, 0, 8003, 9000,
    8001, 9010, 9013, 8012, 10000, 8002, 9011, 3100, 3110, 10010, 9003, 9001, 9012, 9002,
    4100, 5100, 6100, 5110, 10020, 7100, 5101, 6110, 5103, 10030, 8100, 8101, 4110, 5111,
    5113, 8110, 11000, 8103, 12023, 5102, 12021, 12002, 12012, 12022, 9100, 7110, 13023, 15021,
    9101, 5112, 13021, 15020, 8111, 13002, 14000, 13012, 14010, 9110, 8113, 9103, 13022, 14020,
    12001, 8102, 12011, 12020, 10110, 8112, 13001, 13011, 13020, 15000, 12003, 12013, 16020, 9102,
    10120, 9113, 16021, 9112, 17022, 18020, 17021, 13003, 15001, 16000, 13013, 15011, 16010, 16001,
    16011, 19020, 12010, 15010, 9111, 12000, 10100, 10130, 17023, 19021, 17020, 20020, 20021, 11100,
    12123, 12122, 12121, 13000, 17001, 19000, 17002, 18000, 13010, 17011, 19010, 17010, 17012, 18010,
    12102, 17003, 19001, 13122, 13123, 15121, 12112, 13121, 15120, 17013, 19011, 21022, 13102, 21023,
    14100, 20000, 13112, 14110, 20010, 20001, 12101, 21021, 12111, 12120, 12103, 13101, 15100, 12113,
    13111, 15110, 14120, 17000, 21002, 21003, 21000, 13120, 13103, 15101, 16100, 13113, 16110, 15111,
    16101, 16111, 21020, 22020, 20011, 16120, 12100, 12110, 16121, 23023, 23021, 23022, 13110, 17111,
    19110, 21001, 24020, 13100, 17122, 18120, 17123, 17120, 19121, 17102, 18100, 17101, 17112, 18110,
    19100, 21012, 17121, 19120, 17100, 17103, 19101, 20100, 21013, 22000, 17113, 19111, 20120, 20121,
    20110, 21011, 20111, 17110, 21010, 20101, 21102, 21122, 21123, 21112, 23001, 21120, 23002, 23003,
    21110, 21101, 21103, 21121, 22010, 21111, 21113, 24000, 21100, 22100, 23013, 22120, 22110, 23103,
    23011, 23012, 23102, 24010, 23101, 23121, 23122, 24100, 23123, 23113, 23111, 23112, 24120, 24110,
)
CHUNKS = (((0, 0), (0, 3), (0, 1), (0, 2)), ((3, 0), (1, 0), (3, 3), (1, 3)), ((3, 1), (1, 1), (3, 2), (1, 2)), ((2, 0), (2, 3), (2, 1), (2, 2)))


def plan(gather, scatter, weights_in, hid, free_sem, weights, relay, weigh_all):
    def compute(n, k):
        gather[n].compute(k, *weights_in, hid.at[n])

    def begin():
        weigh_all()
        for copy in weights:
            copy.wait()

    def release(n):
        gather[n].send.drain(gather[n].x.at[:, :, :, :, :, pl.ds(0, gather[n].width // 32 * 30)])
        pl.semaphore_signal(free_sem.at[n], inc=1, device_id=other_core(), device_id_type=MESH)
        pl.semaphore_wait(free_sem.at[n], 1)

    steps = (
        (0, begin),
        (1, relay),
        (1, lambda n: gather[n].start()),
        (2, lambda n, h: gather[n].near(h)),
        (2, lambda n, h: gather[n].far(h)),
        (3, lambda n, h, b: gather[n].onward(h, b)),
        (2, lambda n, h: gather[n].joined_near(h)),
        (2, lambda n, h: gather[n].joined_far(h)),
        (3, lambda n, h, b: gather[n].joined(h, b)),
        (3, lambda n, h, b: gather[n].last(h, b)),
        (2, compute),
        (1, release),
        (3, lambda n, q, i: scatter[n].compute(q, i)),
        (3, lambda n, q, i: scatter[n].chip_sum(q, i)),
        (2, lambda n, q: scatter[n].first[q].send_far()),
        (3, lambda n, q, way: scatter[n].first[q].send_direct(way)),
        (3, lambda n, q, k: scatter[n].first[q].pass_on(k)),
        (3, lambda n, q, b: scatter[n].down(q, b)),
        (2, lambda n, q: scatter[n].second[q].send_far()),
        (3, lambda n, q, way: scatter[n].second[q].send_direct(way)),
        (3, lambda n, q, k: scatter[n].second[q].pass_on(k)),
        (3, lambda n, q, k: scatter[n].end(q, k)),
        (2, lambda n, q: scatter[n].share(q)),
        (3, lambda n, q, by: scatter[n].pair(q, by)),
        (2, lambda n, q: scatter[n].close(q)),
    )
    for code in ORDER:
        count, step = steps[code // 1000]
        step(*(code // place % 10 for place in (100, 10, 1)[:count]))


def per_device(tokens, expert_ids, gate_weights, live_counts, w_gate, w_up, w_down):
    count, width = tokens.shape
    depth = w_gate.shape[2]
    rows = count // 2 // STREAMS
    dma = pltpu.SemaphoreType.DMA
    bf16, f32 = jnp.bfloat16, jnp.float32
    is_live = jnp.arange(count, dtype=jnp.int32)[None, :] < live_counts[0]
    ids, gates = expert_ids.T, gate_weights.T
    named = (ids[:, None, :] == jnp.arange(8, dtype=jnp.int32)[None, :, None]) & is_live[None]
    meta = jnp.sum(jnp.where(named, gates[:, None, :], 0.0), axis=0)

    vmem = pl.BlockSpec(memory_space=pltpu.VMEM)
    hbm = pl.BlockSpec(memory_space=pl.ANY)
    n = STREAMS
    bufs = []
    for q in range(3):
        wide = QUARTERS[q]
        one = (rows, 4 * wide) if q == 1 else (4, rows, wide)
        bufs.append(
            [
                pltpu.VMEM(shape, bf16)
                for shape in (
                    (n, 2, 2, *one), (n, 2, 4, *one), (n, 4, *one), (n, 2, 2, rows, wide), (n, 2, 4, rows, wide),
                    (n, 4, rows, wide), (n, rows, wide), (n, 2, rows, wide),
                )
            ]
        )
    mixed, loads = pl.pallas_call(
        moe_kernel,
        out_shape=(
            jax.ShapeDtypeStruct((2, n, rows, width), bf16),
            jax.ShapeDtypeStruct((1, 128), jnp.int32),
        ),
        in_specs=[vmem, vmem, hbm, hbm, hbm],
        out_specs=(vmem, vmem),
        scratch_shapes=[
            pltpu.VMEM((n, 2, 4, 4, 2, rows // 2, width), bf16),
            pltpu.VMEM((width, depth), bf16),
            pltpu.VMEM((width, depth), bf16),
            pltpu.VMEM((depth, width), bf16),
            pltpu.VMEM((4, 4, 8, count), f32),
            pltpu.VMEM((4, 4, count, count), f32),
            pltpu.VMEM((n, 4, 4, 2, rows, depth), bf16),
            pltpu.VMEM((n, 4, 4, rows, width), bf16),
            bufs,
            dma((3,)),
            dma((n, 5)),
            dma((4,)),
            pltpu.SemaphoreType.REGULAR((n,)),
            [
                dma((n, 2)), dma((n, 2)), dma((n, 2, 4)), dma((n, 2, 2)), dma((n, 2, 4)), dma((n, 2, 4)),
                dma((n, len(CHUNKS))),
            ],
            [
                dma((n, 3, 4)), dma((n, 3, 2)), dma((n, 3, 4)), dma((n, 3, 2)), dma((n, 3, 4)),
                dma((n, 3)), dma((n, 3)), dma((n, 3, 3)), dma((n, 3)),
            ],
        ],
        compiler_params=pltpu.CompilerParams(
            collective_id=0, has_side_effects=True, vmem_limit_bytes=VMEM_LIMIT
        ),
        name="moe",
    )(tokens, meta, w_gate[0], w_up[0], w_down[0])
    return (mixed.reshape(count, width), loads[0, :8])


def solution(mesh):
    torus = Mesh(mesh.devices.reshape(4, 4, 4, 2), DP + EXPERT)
    in_specs = (
        P(DP, None),
        P(DP, None),
        P(DP, None),
        P(DP),
        P(EXPERT, None, DP),
        P(EXPERT, None, DP),
        P(EXPERT, DP, None),
    )
    out_specs = (P(DP, None), P())
    return jax.shard_map(
        per_device, mesh=torus, in_specs=in_specs, out_specs=out_specs, check_vma=False
    )
```

time: 303 us -> 114 us (0.38)
  waiting for transfers between devices: 190 us -> 0 us
  Pallas kernels: 0 us -> 107 us
  matrix products: 35.1 us -> 0 us
  blocking collectives: 32.7 us -> 0 us
  between operations: 14.8 us -> 1.29 us
  local copies, waits for them, and re-layouts: 14.1 us -> 3.47 us
  other arithmetic: 10.5 us -> 1.3 us
  starting transfers between devices: 4.58 us -> 0 us
    pallas_call x0 -> x1, Pallas kernels: none -> 107 us  [per_device(): pl.pallas_call(moe_kernel, out_shape=(jax.ShapeDtypeStruct((2, n, rows, w...]
    reduce_scatter x1 -> x0, waiting for transfers between devices: 94.7 us -> none  [per_device(): lax.psum_scatter(jnp.dot(hidden, down_matrix, preferred_element_type=jnp....]
    all_gather x1 -> x0, waiting for transfers between devices: 93.1 us -> none  [per_device(): gathered = lax.all_gather(outbound, DP, axis=0, tiled=True)]
    dot_general x3 -> x0, matrix products: 35.1 us -> none  [the longest x1 21.9 us: per_device(): jnp.dot(hidden, down_matrix, preferred_element_type=jnp.float32)]
    all_to_all x1 -> x0, blocking collectives: 20.2 us -> none  [sum_at_owner(): tiles = lax.all_to_all(split_up(shard, dim, size), axis, 0, 0, tiled=True)]
    psum x2 -> x0, blocking collectives: 12.6 us -> none  [over_axes(): shard = lax.psum(shard, axis)]
    reduce_sum x3 -> x1, other arithmetic: 8.96 us -> 1.3 us  [per_device(): meta = jnp.sum(jnp.where(named, gates[:, None, :], 0.0), axis=0)]
    gather x1 -> x0, local copies, waits for them, and re-layouts: 5.12 us -> none  [per_device(): selected = summed[pick_index].astype(jnp.float32)]
  transfers between devices with their start and end apart: 3 -> 0, of which waited for: 3 -> 0; matrix products, arithmetic and copies ran while one was open for 0% -> 0% of each run, Pallas kernels for 0% -> 0%
where the time goes in v3:
time: 114 us; the launch traced here: 113 us
  Pallas kernels  107 us (94%)
  local copies, waits for them, and re-layouts  3.47 us (3%)
  other arithmetic  1.3 us (1%)
  between operations  1.29 us (1%)
    pallas_call x1, Pallas kernels, per_device(): pl.pallas_call(moe_kernel, out_shape=(jax.ShapeDtypeStruct((2, n, rows, w...  107 us
    unnamed x1, local copies, waits for them, and re-layouts  2.29 us

profile of v3, /device:TPU:1, one launch (start us, length us, event | category | flops | bytes accessed | tf_op | source)
XLA Modules:
  0.0 113.4 jit_solution(2525976586607296203)
XLA Ops:
  1.3 1.3 %select_reduce_fusion.meta = f32[8,128]{1,0:T(8,128)} fusion(f32[2,128]{1,0:T(2,128)} %bitcast.14, s32[2,128]{1,0:T(2,128)} %bitcast.15, pred[128]{0:T(512)(128)(4,1)S(1)} %iota_compare_fusion.1), kind=kLoop, calls=%fused_computation | loop fusion | flops 7168 | bytes 6272 | tf_op jit(solution)/shard_map/reduce_sum | solution.py:510
  2.6 107.4 %moe.1 = (bf16[2,2,32,4096]{3,2,1,0:T(8,128)(2,1)}, s32[1,128]{1,0:T(1,128)}) custom-call(bf16[128,4096]{1,0:T(8,128)(2,1)} %tok.1, f32[8,128]{1,0:T(8,128)} %select_reduce_fusion.meta, bf16[4096,512]{1,0:T(8,128)(2,1)} %bitcast.10, bf16[4096,512]{1,0:T(8,128)(2,1)} %bitcast.11, bf16[512,4096]{1,0:T(8,128)(2,1)} %bitcast.12), custom_call_target="tpu_custom_call" | custom-call | tf_op jit(solution)/shard_map/moe/pallas_call | solution.py:528
  110.0 1.2 %slice_bitcast_fusion = s32[8]{0:T(128)} fusion(s32[1,128]{1,0:T(1,128)} %get-tuple-element.5), kind=kLoop, calls=%fused_computation.3 | loop fusion | bytes 64 | tf_op jit(solution)/shard_map/squeeze | solution.py:564
  111.1 2.3 %copy.11 = bf16[128,4096]{1,0:T(8,128)(2,1)} copy(bf16[128,4096]{1,0:T(8,128)(2,1)} %bitcast.13) | data formatting | bytes 2097152
  (1 shorter events, 0.0 us)

commit v4 on v3

--- a/solution.py
+++ b/solution.py
@@ -394,7 +394,7 @@
 
 
 def moe_kernel(
-    tok, meta, wg_hbm, wu_hbm, wd_hbm, ob, loads, x, wg, wu, wd, m, wcol, hid, s, bufs,
+    tok, ids, gates, live, wg_hbm, wu_hbm, wd_hbm, ob, loads, x, wg, wu, wd, m, wcol, hid, s, bufs,
     wsem, send_sem, meta_sem, free_sem, collect_sems, recv,
 ):
     weights = [
@@ -403,7 +403,14 @@
     ]
     for copy in weights:
         copy.start()
-    m[0, 0] = meta[...]
+    count = tok.shape[0]
+    token = lax.broadcasted_iota(jnp.int32, (8, count), 1)
+    expert = lax.broadcasted_iota(jnp.int32, (8, count), 0)
+    meta = jnp.zeros((8, count), jnp.float32)
+    for k in range(2):
+        named = (jnp.broadcast_to(ids[k : k + 1, :], (8, count)) == expert) & (token < live[0])
+        meta = meta + jnp.where(named, jnp.broadcast_to(gates[k : k + 1, :], (8, count)), 0.0)
+    m[0, 0] = meta
     enter([other_core(), {"x": shifted("x", 2)}] + [{a: shifted(a, by)} for a in ("x", "y", "z") for by in (1, -1)])
     send = Sender(send_sem.at[0, 0])
     gather, scatter = [], []
@@ -429,25 +436,25 @@
 
 
 ORDER = (
-    2000, 1100, 3010, 3000, 5010, 1200, 5000, 4010, 6010, 5013, 8010, 5011, 4000, 5001,
-    1300, 5003, 8000, 7010, 6000, 8013, 8011, 2100, 5012, 7000, 5002, 0, 8003, 9000,
-    8001, 9010, 9013, 8012, 10000, 8002, 9011, 3100, 3110, 10010, 9003, 9001, 9012, 9002,
-    4100, 5100, 6100, 5110, 10020, 7100, 5101, 6110, 5103, 10030, 8100, 8101, 4110, 5111,
-    5113, 8110, 11000, 8103, 12023, 5102, 12021, 12002, 12012, 12022, 9100, 7110, 13023, 15021,
-    9101, 5112, 13021, 15020, 8111, 13002, 14000, 13012, 14010, 9110, 8113, 9103, 13022, 14020,
-    12001, 8102, 12011, 12020, 10110, 8112, 13001, 13011, 13020, 15000, 12003, 12013, 16020, 9102,
-    10120, 9113, 16021, 9112, 17022, 18020, 17021, 13003, 15001, 16000, 13013, 15011, 16010, 16001,
-    16011, 19020, 12010, 15010, 9111, 12000, 10100, 10130, 17023, 19021, 17020, 20020, 20021, 11100,
-    12123, 12122, 12121, 13000, 17001, 19000, 17002, 18000, 13010, 17011, 19010, 17010, 17012, 18010,
-    12102, 17003, 19001, 13122, 13123, 15121, 12112, 13121, 15120, 17013, 19011, 21022, 13102, 21023,
-    14100, 20000, 13112, 14110, 20010, 20001, 12101, 21021, 12111, 12120, 12103, 13101, 15100, 12113,
-    13111, 15110, 14120, 17000, 21002, 21003, 21000, 13120, 13103, 15101, 16100, 13113, 16110, 15111,
-    16101, 16111, 21020, 22020, 20011, 16120, 12100, 12110, 16121, 23023, 23021, 23022, 13110, 17111,
-    19110, 21001, 24020, 13100, 17122, 18120, 17123, 17120, 19121, 17102, 18100, 17101, 17112, 18110,
-    19100, 21012, 17121, 19120, 17100, 17103, 19101, 20100, 21013, 22000, 17113, 19111, 20120, 20121,
-    20110, 21011, 20111, 17110, 21010, 20101, 21102, 21122, 21123, 21112, 23001, 21120, 23002, 23003,
-    21110, 21101, 21103, 21121, 22010, 21111, 21113, 24000, 21100, 22100, 23013, 22120, 22110, 23103,
-    23011, 23012, 23102, 24010, 23101, 23121, 23122, 24100, 23123, 23113, 23111, 23112, 24120, 24110,
+    2000, 1100, 3000, 3010, 1200, 5000, 5010, 4000, 5003, 6010, 6000, 8000, 5001, 4010,
+    5011, 1300, 5013, 8010, 7000, 8003, 8001, 2100, 7010, 5002, 5012, 9000, 9010, 8011,
+    0, 10000, 8012, 8013, 9003, 9001, 8002, 3110, 5110, 3100, 5100, 10010, 6110, 9002,
+    9011, 9012, 9013, 10020, 10030, 6100, 4100, 5103, 5101, 8100, 8110, 4110, 5111, 5113,
+    11000, 12022, 12012, 12021, 7100, 12002, 9110, 13022, 14020, 5102, 13012, 14010, 8103, 9100,
+    13021, 15020, 12023, 7110, 8101, 13002, 14000, 5112, 12001, 8111, 12011, 10100, 9101, 8113,
+    9103, 13001, 15000, 13023, 15021, 16020, 13011, 8102, 15010, 12020, 10110, 13020, 8112, 9113,
+    12013, 9111, 16021, 12003, 17022, 18020, 10120, 17023, 17021, 19020, 17020, 9102, 9112, 20020,
+    20021, 13003, 15001, 16000, 16001, 19021, 13013, 15011, 16010, 10130, 21022, 21023, 21020, 16011,
+    11100, 12122, 12121, 12102, 12112, 12123, 21021, 13122, 14120, 13121, 15120, 12101, 13102, 14100,
+    12111, 13112, 14110, 13123, 15121, 12120, 12113, 13101, 15100, 12103, 16120, 13120, 22020, 13111,
+    15110, 13113, 15111, 16121, 12000, 13103, 15101, 16100, 12010, 12110, 16110, 13000, 17001, 19000,
+    17002, 17003, 19001, 17000, 16101, 18000, 17121, 23023, 13110, 17122, 18120, 23021, 13010, 17012,
+    17011, 17013, 19011, 19010, 17123, 18010, 23022, 17120, 19120, 12100, 24020, 19121, 17010, 16111,
+    20000, 20001, 13100, 17102, 18100, 17101, 19100, 17112, 18110, 20120, 17100, 21002, 17111, 19110,
+    21003, 21000, 20121, 17103, 19101, 20100, 20101, 17110, 20010, 21122, 20011, 21001, 17113, 19111,
+    20110, 21120, 21102, 21123, 21012, 21121, 21103, 21010, 20111, 21112, 21101, 22000, 21013, 21100,
+    21011, 22120, 21110, 21113, 21111, 22100, 23123, 23001, 23002, 23003, 22010, 23122, 24000, 23121,
+    23103, 22110, 24120, 23102, 23101, 23013, 23012, 23011, 24100, 23113, 24010, 23111, 23112, 24110,
 )
 CHUNKS = (((0, 0), (0, 3), (0, 1), (0, 2)), ((3, 0), (1, 0), (3, 3), (1, 3)), ((3, 1), (1, 1), (3, 2), (1, 2)), ((2, 0), (2, 3), (2, 1), (2, 2)))
 
@@ -504,11 +511,6 @@
     rows = count // 2 // STREAMS
     dma = pltpu.SemaphoreType.DMA
     bf16, f32 = jnp.bfloat16, jnp.float32
-    is_live = jnp.arange(count, dtype=jnp.int32)[None, :] < live_counts[0]
-    ids, gates = expert_ids.T, gate_weights.T
-    named = (ids[:, None, :] == jnp.arange(8, dtype=jnp.int32)[None, :, None]) & is_live[None]
-    meta = jnp.sum(jnp.where(named, gates[:, None, :], 0.0), axis=0)
-
     vmem = pl.BlockSpec(memory_space=pltpu.VMEM)
     hbm = pl.BlockSpec(memory_space=pl.ANY)
     n = STREAMS
@@ -531,7 +533,7 @@
             jax.ShapeDtypeStruct((2, n, rows, width), bf16),
             jax.ShapeDtypeStruct((1, 128), jnp.int32),
         ),
-        in_specs=[vmem, vmem, hbm, hbm, hbm],
+        in_specs=[vmem, vmem, vmem, pl.BlockSpec(memory_space=pltpu.SMEM), hbm, hbm, hbm],
         out_specs=(vmem, vmem),
         scratch_shapes=[
             pltpu.VMEM((n, 2, 4, 4, 2, rows // 2, width), bf16),
@@ -560,7 +562,7 @@
             collective_id=0, has_side_effects=True, vmem_limit_bytes=VMEM_LIMIT
         ),
         name="moe",
-    )(tokens, meta, w_gate[0], w_up[0], w_down[0])
+    )(tokens, expert_ids.T, gate_weights.T, live_counts, w_gate[0], w_up[0], w_down[0])
     return (mixed.reshape(count, width), loads[0, :8])
 
 

time: 114 us -> 111 us (0.974)
  other arithmetic: 1.3 us -> 0 us
    reduce_sum x1 -> x0, other arithmetic: 1.3 us -> none  [per_device(): meta = jnp.sum(jnp.where(named, gates[:, None, :], 0.0), axis=0)]
    pallas_call x1, Pallas kernels: 107 us -> 106 us  [per_device(): pl.pallas_call(moe_kernel, out_shape=(jax.ShapeDtypeStruct((2, n, rows, w...]
where the time goes in v4:
time: 111 us
  Pallas kernels  106 us (95%)
  local copies, waits for them, and re-layouts  3.4 us (3%)
  between operations  1.29 us (1%)
    pallas_call x1, Pallas kernels, per_device(): pl.pallas_call(moe_kernel, out_shape=(jax.ShapeDtypeStruct((2, n, rows, w...  106 us
    unnamed x1, local copies, waits for them, and re-layouts  2.29 us

profile of v4, /device:TPU:1, one launch (start us, length us, event | category | flops | bytes accessed | tf_op | source)
XLA Modules:
  0.0 110.8 jit_solution(4797119410058600988)
XLA Ops:
  1.3 106.1 %moe.1 = (bf16[2,2,32,4096]{3,2,1,0:T(8,128)(2,1)}, s32[1,128]{1,0:T(1,128)}) custom-call(bf16[128,4096]{1,0:T(8,128)(2,1)} %tok.1, s32[2,128]{1,0:T(2,128)} %bitcast.12, f32[2,128]{1,0:T(2,128)} %bitcast.13, s32[1]{0:T(128)S(6)} %copy.10.live, bf16[4096,512]{1,0:T(8,128)(2,1)} %bitcast.8, bf16[4096,512]{1,0:T(8,128)(2,1)} %bitcast.9, bf16[512,4096]{1,0:T(8,128)(2,1)} %bitcast.10), custom_call_target="tpu_custom_call" | custom-call | tf_op jit(solution)/shard_map/moe/pallas_call | solution.py:530
  107.4 1.1 %slice_bitcast_fusion = s32[8]{0:T(128)} fusion(s32[1,128]{1,0:T(1,128)} %get-tuple-element.5), kind=kLoop, calls=%fused_computation | loop fusion | bytes 64 | tf_op jit(solution)/shard_map/squeeze | solution.py:566
  108.5 2.3 %copy.11 = bf16[128,4096]{1,0:T(8,128)(2,1)} copy(bf16[128,4096]{1,0:T(8,128)(2,1)} %bitcast.11) | data formatting | bytes 2097152

commit v5 on v4

--- a/solution.py
+++ b/solution.py
@@ -426,8 +426,6 @@
         scatter.append(Scatter(send_sem.at[n, pl.ds(2, 3)], hid.at[n], wd, x.at[n], s.at[n], ob.at[:, n], parts, sems))
 
     pass_meta(m, send, meta_sem, 0)
-    for each in gather:
-        each.fill()
     relay = functools.partial(pass_meta, m, send, meta_sem)
     plan(gather, scatter, (wg, wu, wcol), hid, free_sem, weights, relay, lambda: weigh(m, meta_sem, wcol, loads))
     send.drain(wcol.at[0, pl.ds(0, 1), pl.ds(0, 120)])
@@ -464,6 +462,8 @@
         gather[n].compute(k, *weights_in, hid.at[n])
 
     def begin():
+        for each in gather:
+            each.fill()
         weigh_all()
         for copy in weights:
             copy.wait()

time: 111 us -> 111 us (level)
  no operation moved by 1% of the time
where the time goes in v5:
time: 111 us
  Pallas kernels  106 us (95%)
  local copies, waits for them, and re-layouts  3.4 us (3%)
  between operations  1.29 us (1%)
    pallas_call x1, Pallas kernels, per_device(): pl.pallas_call(moe_kernel, out_shape=(jax.ShapeDtypeStruct((2, n, rows, w...  106 us
    unnamed x1, local copies, waits for them, and re-layouts  2.29 us

profile of v5, /device:TPU:1, one launch (start us, length us, event | category | flops | bytes accessed | tf_op | source)
XLA Modules:
  0.0 110.8 jit_solution(5193311055367898157)
XLA Ops:
  1.3 106.1 %moe.1 = (bf16[2,2,32,4096]{3,2,1,0:T(8,128)(2,1)}, s32[1,128]{1,0:T(1,128)}) custom-call(bf16[128,4096]{1,0:T(8,128)(2,1)} %tok.1, s32[2,128]{1,0:T(2,128)} %bitcast.12, f32[2,128]{1,0:T(2,128)} %bitcast.13, s32[1]{0:T(128)S(6)} %copy.10.live, bf16[4096,512]{1,0:T(8,128)(2,1)} %bitcast.8, bf16[4096,512]{1,0:T(8,128)(2,1)} %bitcast.9, bf16[512,4096]{1,0:T(8,128)(2,1)} %bitcast.10), custom_call_target="tpu_custom_call" | custom-call | tf_op jit(solution)/shard_map/moe/pallas_call | solution.py:530
  107.4 1.1 %slice_bitcast_fusion = s32[8]{0:T(128)} fusion(s32[1,128]{1,0:T(1,128)} %get-tuple-element.5), kind=kLoop, calls=%fused_computation | loop fusion | bytes 64 | tf_op jit(solution)/shard_map/squeeze | solution.py:566
  108.5 2.3 %copy.11 = bf16[128,4096]{1,0:T(8,128)(2,1)} copy(bf16[128,4096]{1,0:T(8,128)(2,1)} %bitcast.11) | data formatting | bytes 2097152
